TPU v7x, 128 devices: a whole 4x4x4 slice. The times are simulated.
128 devices in a mesh: wide: 64 (over x, y_hi, z, core), pair: 2 (over y_lo).
Axes of the slice: x: 4, y: 4 (y_hi: 2, y_lo: 2; y = y_hi * 2 + y_lo), z: 4, core: 2. Of those that a mesh axis runs over, the one named last changes fastest.
Arguments:
- pooled_b: bfloat16 [64, 64, 512, 128], P('wide', None, 'pair'), may hold values from -6 to 6
- dense_output_second: bfloat16 [32768, 128], P(('wide', 'pair')), may hold values from -4 to 4
- counts_b: int32 [32768, 26], P(('wide', 'pair')), may hold values from 1 to 8
- slot_of: int32 [64], replicated, may hold values from 0 to 63, each once
- stacked_a: bfloat16 [32768, 3456], P(('wide', 'pair')), may hold values from -4 to 4
- upstream_a: bfloat16 [32768, 3456], P(('wide', 'pair')), may hold values from -6 to 6
- counts_a: int32 [32768, 26], P(('wide', 'pair')), may hold values from 1 to 8
- down_projection: bfloat16 [3456, 512], P('wide'), may hold values from -0.109375 to 0.109375
- proj_up: bfloat16 [512, 3456], P(None, 'wide'), may hold values from -0.25 to 0.25
- cross_layer_bias: bfloat16 [3456], P('wide'), may hold values from -3 to 3
Outputs:
- crossed_b: bfloat16 [32768, 3456], P(('wide', 'pair'))
- dense_grad_a: bfloat16 [32768, 128], P(('wide', 'pair'))
- pooled_grad_a: bfloat16 [64, 64, 512, 128], P('wide', None, 'pair')
- grad_down: float32 [3456, 512], P('wide')
- grad_up: float32 [512, 3456], P(None, 'wide')
- grad_bias: float32 [3456], P('wide')
Inputs may be any that keep to these rules, and one draw needn't show every extreme that they name: slot_of holds every slot once; its first 26 entries are the slots of tables 0 to 25, the rest are unused. Slot s lies on index s // 1 of wide.
All inputs are finite; a program needn't handle non-finite values.
Results may differ from a plain program's by a relative error of at most 0.0075.
Values may be sent and summed in bfloat16 or wider, within the bound.
A program may use at most 128 MiB of HBM per device.

v0:
```python
import jax
import jax.numpy as jnp
from jax import lax
from jax.sharding import PartitionSpec as P


def gather_turned(arrays, axis, dims):
    turned = [jnp.moveaxis(a, dim, 0) for a, dim in zip(arrays, dims)]
    widths = [t[0].size for t in turned]
    both = jnp.concatenate([t.reshape(-1, w) for t, w in zip(turned, widths)], axis=1)
    filled = lax.all_gather(both, axis, axis=0, tiled=True)
    blocks = jnp.split(filled, [sum(widths[:k]) for k in range(1, len(widths))], axis=1)
    return tuple(
        (
            jnp.moveaxis(b.reshape(-1, *t.shape[1:]), 0, dim)
            for b, t, dim in zip(blocks, turned, dims)
        )
    )


def table_means(slot_rows, lookup_count, table_slots):
    picked = jnp.take(slot_rows, table_slots, axis=0).astype(jnp.float32)
    scaled = picked / jnp.transpose(lookup_count).astype(jnp.float32)[:, :, None]
    return jnp.transpose(scaled, (1, 0, 2)).reshape(scaled.shape[1], -1).astype(jnp.bfloat16)


def cross_forward(stacked, down, up):
    low_rank = jnp.dot(stacked, down, preferred_element_type=jnp.float32).astype(jnp.bfloat16)
    projected = jnp.dot(low_rank, up, preferred_element_type=jnp.float32)
    return (low_rank, projected)


def crossed_output(stacked, projected, bias):
    stacked_wide = stacked.astype(jnp.float32)
    return (stacked_wide * (projected + bias.astype(jnp.float32)) + stacked_wide).astype(
        jnp.bfloat16
    )


def cross_backward(stacked, upstream, lookup_count, down, up, bias, feature_index):
    low_rank, projected = cross_forward(stacked, down, up)
    stacked_wide = stacked.astype(jnp.float32)
    upstream_wide = upstream.astype(jnp.float32)
    scale_grad = upstream_wide * stacked_wide
    grad_bias = jnp.sum(scale_grad, axis=0)
    proj_grad = scale_grad.astype(jnp.bfloat16)
    over_rows = (((0,), (0,)), ((), ()))
    over_cols = (((1,), (1,)), ((), ()))
    grad_up = lax.dot_general(low_rank, proj_grad, over_rows, preferred_element_type=jnp.float32)
    low_grad = lax.dot_general(proj_grad, up, over_cols, preferred_element_type=jnp.float32).astype(
        jnp.bfloat16
    )
    grad_down = lax.dot_general(stacked, low_grad, over_rows, preferred_element_type=jnp.float32)
    input_grad = upstream_wide * (projected + bias.astype(jnp.float32)) + upstream_wide
    input_grad = input_grad + lax.dot_general(
        low_grad, down, over_cols, preferred_element_type=jnp.float32
    )
    rows = stacked.shape[0]
    dense_gradient = input_grad[:, :feature_index].astype(jnp.bfloat16)
    table_gradient = (
        input_grad[:, feature_index:].reshape(rows, -1, feature_index)
        / lookup_count.astype(jnp.float32)[:, :, None]
    )
    table_gradient = jnp.transpose(table_gradient, (1, 0, 2)).astype(jnp.bfloat16)
    return (dense_gradient, table_gradient, grad_down, grad_up, grad_bias)


def local(
    pooled_b,
    dense_output_second,
    counts_b,
    slot_of,
    stacked_a,
    upstream_a,
    counts_a,
    down_projection,
    proj_up,
    cross_layer_bias,
):
    feature_index = dense_output_second.shape[1]
    tables = counts_b.shape[1]
    table_slots = slot_of[:tables]
    arrived = lax.all_to_all(pooled_b, "wide", split_axis=1, concat_axis=0, tiled=True)
    slot_count = arrived.shape[0]
    samples = arrived.shape[2]
    down, up, bias = gather_turned((down_projection, proj_up, cross_layer_bias), "wide", (0, 1, 0))
    slot_rows = arrived.reshape(slot_count, samples, feature_index)
    stacked_b = jnp.concatenate(
        [dense_output_second, table_means(slot_rows, counts_b, table_slots)], axis=1
    )
    low_rank, projected = cross_forward(stacked_b, down, up)
    crossed_b = crossed_output(stacked_b, projected, bias)
    dense_gradient, table_gradient, grad_down, grad_up, grad_bias = cross_backward(
        stacked_a, upstream_a, counts_a, down, up, bias, feature_index
    )
    slot_selector = (
        table_slots[None, :] == jnp.arange(slot_count, dtype=jnp.int32)[:, None]
    ).astype(jnp.bfloat16)
    slot_grad = jnp.einsum(
        "qv,vxk->qxk", slot_selector, table_gradient, preferred_element_type=jnp.float32
    ).astype(jnp.bfloat16)
    returned = lax.all_to_all(
        slot_grad.reshape(slot_count, 1, samples, feature_index),
        "wide",
        split_axis=0,
        concat_axis=1,
        tiled=True,
    )
    halves = (
        lax.psum_scatter(grad_down, ("wide", "pair"), scatter_dimension=0, tiled=True),
        lax.psum_scatter(grad_up, ("wide", "pair"), scatter_dimension=1, tiled=True),
        lax.psum_scatter(grad_bias, ("wide", "pair"), scatter_dimension=0, tiled=True),
    )
    summed = tuple(
        (
            part.astype(jnp.float32)
            for part in gather_turned(
                (
                    halves[0].astype(jnp.bfloat16),
                    halves[1].astype(jnp.bfloat16),
                    halves[2].astype(jnp.bfloat16),
                ),
                "pair",
                (0, 1, 0),
            )
        )
    )
    return (crossed_b, dense_gradient, returned, summed[0], summed[1], summed[2])


def solution(mesh):
    return jax.shard_map(
        local,
        mesh=mesh,
        in_specs=(
            P("wide", None, "pair", None),
            P(("wide", "pair"), None),
            P(("wide", "pair"), None),
            P(),
            P(("wide", "pair"), None),
            P(("wide", "pair"), None),
            P(("wide", "pair"), None),
            P("wide", None),
            P(None, "wide"),
            P("wide"),
        ),
        out_specs=(
            P(("wide", "pair"), None),
            P(("wide", "pair"), None),
            P("wide", None, "pair", None),
            P("wide", None),
            P(None, "wide"),
            P("wide"),
        ),
        check_vma=False,
    )
```

profile of v0, /device:TPU:1, one launch (start us, length us, event | category | flops | bytes accessed | tf_op | source)
XLA Modules:
  0.0 374.6 jit_solution(4722316046198100531)
XLA Ops:
  8.0 1.5 maximum_bitcast_fusion
  9.5 12.7 %all-to-all-start = ((bf16[1,64,256,128]{3,2,0,1:T(8,128)(2,1)}), bf16[1,64,256,128]{3,2,0,1:T(8,128)(2,1)}, u32[]{:S(2)}, u32[]{:S(2)}) async-start(bf16[1,64,256,128]{3,2,0,1:T(8,128)(2,1)} %bitcast.44), calls=%async_computation | async-start | bytes 8388608 | tf_op jit(solution)/shard_map/all_to_all | solution.py:83
  22.8 109.4 %all-gather.4.cloned.1.call-done = bf16[64,54,1025]{2,1,0:T(8,128)(2,1)} async-done(((bf16[1,54,1025]{2,1,0:T(8,128)(2,1)}), bf16[64,54,1025]{2,1,0:T(8,128)(2,1)}) %all-gather.4.cloned.1.call-update) | async-done | bytes 7084816 | tf_op jit(solution)/shard_map/all_gather | solution.py:11
  132.2 10.4 %reshape.72 = bf16[3456,1025]{1,0:T(8,128)(2,1)} reshape(bf16[64,54,1025]{2,1,0:T(8,128)(2,1)} %all-gather.4.cloned.1.call-done) | data formatting | bytes 14169600
  144.1 3.3 fusion.23
  152.0 1.8 copy-done.2
  153.8 2.0 slice.16
  155.7 5.0 %copy.51 = f32[256,3328]{0,1:T(8,128)} copy(f32[256,3328]{1,0:T(8,128)} %slice.16) | data formatting | bytes 6815744 | tf_op jit(solution)/shard_map/slice | solution.py:61
  160.7 3.6 fusion.17
  164.3 4.4 %copy.52 = bf16[26,256,128]{2,0,1:T(8,128)(2,1)} copy(bf16[26,256,128]{1,2,0:T(8,128)(2,1)} %fusion.17) | data formatting | bytes 3407872 | tf_op jit(solution)/shard_map/convert_element_type | solution.py:64
  168.7 2.9 convert_bitcast_fusion
  171.7 4.7 %copy.53 = bf16[64,1,256,128]{3,2,1,0:T(8,128)(2,1)} copy(bf16[64,1,256,128]{3,0,2,1:T(8,128)(2,1)S(1)} %convert_bitcast_fusion) | data formatting | bytes 8388608 | tf_op jit(solution)/shard_map/reshape | solution.py:103
  176.4 6.3 %all-to-all-start.1 = ((bf16[64,1,256,128]{3,2,1,0:T(8,128)(2,1)}), bf16[64,1,256,128]{3,2,1,0:T(8,128)(2,1)}, u32[]{:S(2)}, u32[]{:S(2)}) async-start(bf16[64,1,256,128]{3,2,1,0:T(8,128)(2,1)} %copy.53), calls=%async_computation.1 | async-start | bytes 8388608 | tf_op jit(solution)/shard_map/all_to_all | solution.py:102
  186.4 4.3 %gather_fusion = bf16[26,256,128]{2,1,0:T(8,128)(2,1)} fusion(bf16[64,256,128]{2,1,0:T(8,128)(2,1)} %bitcast.1, s32[1024]{0:T(1024)} %pad_clamp_fusion), kind=kCustom, calls=%fused_computation | custom fusion | bytes 3407976 | tf_op jit(solution)/shard_map/jit(_take)/gather | solution.py:22
  190.7 3.2 fusion.5
  193.9 3.8 %copy.48 = bf16[256,26,128]{0,2,1:T(8,128)(2,1)} copy(bf16[256,26,128]{2,0,1:T(8,128)(2,1)} %fusion.5) | data formatting | bytes 3407872 | tf_op jit(solution)/shard_map/convert_element_type | solution.py:24
  197.7 3.8 %copy.49 = bf16[256,3328]{1,0:T(8,128)(2,1)} copy(bf16[256,3328]{0,1:T(8,128)(2,1)} %bitcast.43) | data formatting | bytes 3407872 | tf_op jit(solution)/shard_map/convert_element_type | solution.py:24
  201.4 1.5 slice.19
  203.0 5.0 %fusion.29 = f32[512,3456]{1,0:T(8,128)} fusion(bf16[512,256]{1,0:T(8,128)(2,1)} %copy-done.7, bf16[256,3456]{1,0:T(8,128)(2,1)S(1)} %copy-done.1, bf16[256,3456]{1,0:T(8,128)(2,1)S(1)} %copy-done.3), kind=kOutput, calls=%fused_computation.32 | convolution fusion | flops 909508608 | bytes 10878976 | tf_op jit(solution)/shard_map/dot_general | solution.py:49
  207.9 4.1 %convolution_bitcast_fusion = f32[3456,512]{0,1:T(8,128)} fusion(bf16[256,512]{1,0:T(8,128)(2,1)S(1)} %copy-done.6, bf16[256,3456]{1,0:T(8,128)(2,1)S(1)} %copy-done.1), kind=kOutput, calls=%fused_computation.1 | convolution fusion | flops 905969664 | bytes 9109504 | tf_op jit(solution)/shard_map/dot_general | solution.py:53
  212.1 136.6 %all-reduce.5 = (bf16[3456]{0:T(1024)(128)(2,1)S(1)}, bf16[512,3456]{1,0:T(8,128)(2,1)}, bf16[3456,512]{0,1:T(8,128)(2,1)}) all-reduce(f32[3456]{0:T(1024)S(1)} %fusion.6, f32[512,3456]{1,0:T(8,128)} %fusion.29, f32[3456,512]{0,1:T(8,128)} %convolution_bitcast_fusion), channel_id=4, replica_groups=mesh['wide'=64,'pair'=2] {'wide','pair'}, use_global_device_ids=true, to_apply=%region_3.4.clone | all-reduce | flops 3542400 | bytes 21254400
  351.2 3.9 %all-gather.1 = bf16[2,27,1025]{2,1,0:T(8,128)(2,1)S(1)} all-gather(bf16[1,27,1025]{2,1,0:T(8,128)(2,1)S(1)} %maximum_bitcast_fusion.1), channel_id=1, replica_groups=mesh['wide'=64,'pair'=2] {'pair'}, dimensions={0}, use_global_device_ids=true | all-gather | bytes 166050 | tf_op jit(solution)/shard_map/all_gather | solution.py:11
  356.5 6.6 %fusion.4 = bf16[256,3456]{1,0:T(8,128)(2,1)} fusion(bf16[3456,1025]{1,0:T(8,128)(2,1)} %reshape.72, f32[3456]{0:T(1024)S(1)} %copy-done.10, bf16[256,3328]{1,0:T(8,128)(2,1)S(1)} %copy-done.4, bf16[256,128]{1,0:T(8,128)(2,1)S(1)} %copy-done.12), kind=kOutput, calls=%fused_computation.9 | convolution fusion | flops 1822687232 | bytes 12402688 | tf_op jit(solution)/shard_map/dot_general | solution.py:29
  363.1 4.7 %copy.70 = bf16[1,64,256,128]{3,2,1,0:T(8,128)(2,1)} copy(bf16[1,64,256,128]{3,2,1,0:T(8,128)(2,1)} %bitcast.11) | data formatting | bytes 8388608
  (49 shorter events, 15.0 us)
Async XLA Ops:
  7.2 125.0 %all-gather.4.cloned.1.call-start = ((), (), s32[]{:S(2)}) async-start(), calls=%async_computation.2 | async-start | bytes 8386560 | tf_op jit(solution)/shard_map/all_gather | solution.py:11
  9.5 12.7 %copy-start.8 = (s32[256,26]{0,1:T(8,128)S(1)}, s32[256,26]{0,1:T(8,128)}, u32[]{:S(2)}) copy-start(s32[256,26]{0,1:T(8,128)} %param.16) | copy-start | bytes 79876
  9.5 166.9 %all-to-all-start = ((bf16[1,64,256,128]{3,2,0,1:T(8,128)(2,1)}), bf16[1,64,256,128]{3,2,0,1:T(8,128)(2,1)}, u32[]{:S(2)}, u32[]{:S(2)}) async-start(bf16[1,64,256,128]{3,2,0,1:T(8,128)(2,1)} %bitcast.44), calls=%async_computation | async-start | bytes 8388608 | tf_op jit(solution)/shard_map/all_to_all | solution.py:83
  22.8 121.3 %copy-start.1 = (bf16[256,3456]{1,0:T(8,128)(2,1)S(1)}, bf16[256,3456]{1,0:T(8,128)(2,1)}, u32[]{:S(2)}) copy-start(bf16[256,3456]{1,0:T(8,128)(2,1)} %param.14) | copy-start | bytes 5308420
  132.2 15.3 %copy-start.3 = (bf16[256,3456]{1,0:T(8,128)(2,1)S(1)}, bf16[256,3456]{1,0:T(8,128)(2,1)}, u32[]{:S(2)}) copy-start(bf16[256,3456]{1,0:T(8,128)(2,1)} %param.15) | copy-start | bytes 5308420
  144.1 3.3 copy-start.9
  144.1 4.3 %copy-start = (bf16[3456,1025]{1,0:T(8,128)(2,1)S(1)}, bf16[3456,1025]{1,0:T(8,128)(2,1)}, u32[]{:S(2)}) copy-start(bf16[3456,1025]{1,0:T(8,128)(2,1)} %reshape.72) | copy-start | bytes 21254404
  148.5 1.2 copy-start.7
  150.8 1.2 copy-start.5
  152.0 1.8 copy-start.2
  160.7 8.0 %copy-start.11 = (s32[64]{0:T(128)S(1)}, s32[64]{0:T(128)}, u32[]{:S(2)}) copy-start(s32[64]{0:T(128)} %param.13) | copy-start | bytes 772
  176.4 186.7 %all-to-all-start.1 = ((bf16[64,1,256,128]{3,2,1,0:T(8,128)(2,1)}), bf16[64,1,256,128]{3,2,1,0:T(8,128)(2,1)}, u32[]{:S(2)}, u32[]{:S(2)}) async-start(bf16[64,1,256,128]{3,2,1,0:T(8,128)(2,1)} %copy.53), calls=%async_computation.1 | async-start | bytes 8388608 | tf_op jit(solution)/shard_map/all_to_all | solution.py:102
  203.0 5.0 %copy-start.6 = (bf16[256,512]{1,0:T(8,128)(2,1)S(1)}, bf16[256,512]{1,0:T(8,128)(2,1)}, u32[]{:S(2)}) copy-start(bf16[256,512]{1,0:T(8,128)(2,1)} %copy-done.5) | copy-start | bytes 786436
  212.0 144.4 %copy-start.4 = (bf16[256,3328]{1,0:T(8,128)(2,1)S(1)}, bf16[256,3328]{1,0:T(8,128)(2,1)}, u32[]{:S(2)}) copy-start(bf16[256,3328]{1,0:T(8,128)(2,1)} %copy.49) | copy-start | bytes 5111812
  212.0 144.4 %copy-start.10 = (f32[3456]{0:T(1024)S(1)}, f32[3456]{0:T(1024)}, u32[]{:S(2)}) copy-start(f32[3456]{0:T(1024)} %copy-done.9) | copy-start | bytes 41476
  212.1 144.4 %copy-start.12 = (bf16[256,128]{1,0:T(8,128)(2,1)S(1)}, bf16[256,128]{1,0:T(8,128)(2,1)}, u32[]{:S(2)}) copy-start(bf16[256,128]{1,0:T(8,128)(2,1)} %param.11) | copy-start | bytes 196612
Sparse Core Ops, SparseCore 0:
  11.7 120.4 all-gather.3
where the time goes:
time: 376 us; the launch traced here: 375 us
  blocking collectives  140 us (37%)
  waiting for transfers between devices  109 us (29%)
  local copies, waits for them, and re-layouts  50.8 us (14%)
  matrix products  25.4 us (7%)
  starting transfers between devices  19 us (5%)
  other arithmetic  15.4 us (4%)
  between operations  14.2 us (4%)
    unnamed x1, blocking collectives  137 us
    all_gather x1, waiting for transfers between devices, gather_turned(): filled = lax.all_gather(both, axis, axis=0, tiled=True)  109 us
    unnamed x30, local copies, waits for them, and re-layouts  19 us
    all_to_all x1, starting transfers between devices, local(): lax.all_to_all(pooled_b, 'wide', split_axis=1, concat_axis=0, tiled=True)  12.7 us
    dot_general x2, matrix products, cross_forward(): projected = jnp.dot(low_rank, up, preferred_element_type=jnp.float32)  7.78 us
    convert_element_type x2, local copies, waits for them, and re-layouts, table_means(): jnp.transpose(scaled, (1, 0, 2)).reshape(scaled.shape[1], -1)  7.54 us
  transfers between devices with their start and end apart: 3, of which 1 were waited for; matrix products, arithmetic and copies ran while one was open for 22% of the time, Pallas kernels for 0%

commit v1 on v0

v1 whole, which is shorter than its diff:
```python
import functools

import jax
import jax.numpy as jnp
from jax import lax
from jax.experimental import pallas as pl
from jax.experimental.pallas import tpu as pltpu
from jax.sharding import PartitionSpec as P

MESH = pl.DeviceIdType.MESH
F32 = jnp.float32
BF16 = jnp.bfloat16

ROWS = 54
PAD = 56
RANK = 512
E = 128
TABLES = 26
SLOTS = 64
SAMP = 256
WIDTH = 3456
BLK = 384
OVER_ROWS = (((0,), (0,)), ((), ()))
OVER_COLS = (((1,), (1,)), ((), ()))


def place():
    w = lax.axis_index("wide")
    yl = lax.axis_index("pair")
    return w // 16, (w // 8) % 2, yl, (w // 2) % 4, w % 2


def device(x, yh, yl, z, c):
    return (((x * 2 + yh) * 4 + z) * 2 + c, yl)


def along_a(x, yh, yl, z, c, d):
    return device((x + d * (1 - c)) % 4, yh, yl, (z + d * c) % 4, c)


def along_b(x, yh, yl, z, c, d):
    return device((x + d * c) % 4, yh, yl, (z + d * (1 - c)) % 4, c)


def meet(devices):
    barrier = pltpu.get_barrier_semaphore()
    for d in devices:
        pl.semaphore_signal(barrier, inc=1, device_id=d, device_id_type=MESH)
    pl.semaphore_wait(barrier, len(devices))


def gather_kernel(shard, full, send, recv, local_sem):
    x, yh, yl, z, c = place()
    o = 1 - c
    b = z * o + x * c
    a = x * o + z * c
    k = yh * 2 + c
    sib = device(x, yh, yl, z, o)
    part = [device(x, 1 - yh, 1 - yl, z, i) for i in range(2)]
    a_next, a_prev = along_a(x, yh, yl, z, c, 1), along_a(x, yh, yl, z, c, 3)
    b_next, b_prev = along_b(x, yh, yl, z, c, 1), along_b(x, yh, yl, z, c, 3)
    meet([sib, part[0], part[1], a_next, a_prev, b_next, b_prev])
    n = [0]
    started = []

    def copy(src, dst, to, slot):
        cp = pltpu.make_async_remote_copy(
            src_ref=src,
            dst_ref=dst,
            send_sem=send.at[n[0]],
            recv_sem=recv.at[slot],
            device_id=to,
            device_id_type=MESH,
        )
        n[0] += 1
        started.append(cp)
        cp.start()
        return cp

    mine = pltpu.make_async_copy(shard.at[c], full.at[c, b, a, k], local_sem)
    mine.start()
    s1 = []
    for i in range(2):
        bi, ai = (z, x) if i == 0 else (x, z)
        slot = 1 + (c + i) % 2
        s1.append(copy(shard.at[i], full.at[i, bi, ai, k], part[i], slot))
    s1.append(copy(shard.at[o], full.at[o, a, b, k], sib, 0))
    mine.wait()
    for cp in s1:
        cp.wait_recv()
    a_m, a_p, a_o = (a + 3) % 4, (a + 1) % 4, (a + 2) % 4
    b_m, b_p, b_o = (b + 3) % 4, (b + 1) % 4, (b + 2) % 4
    lo, hi = pl.ds(0, 2), pl.ds(2, 2)

    def block(bb, aa):
        return full.at[c, bb, aa]

    def half(bb, aa, h):
        return full.at[c, bb, aa, h]

    up = copy(block(b, a), block(b, a), a_next, 3)
    down = copy(block(b, a), block(b, a), a_prev, 4)
    outer = []

    def out(j, aa):
        outer.append(
            (
                aa,
                copy(block(b, aa), block(b, aa), b_next, 7 + 4 * j),
                copy(block(b, aa), block(b, aa), b_prev, 8 + 4 * j),
                9 + 4 * j,
            )
        )

    across = []

    def over(bb, aa, j):
        across.append(copy(block(bb, aa), block(bb, aa), sib, 23 + j))

    out(0, a)
    up.wait_recv()
    up2 = copy(half(b, a_m, lo), half(b, a_m, lo), a_next, 5)
    out(1, a_m)
    down.wait_recv()
    down2 = copy(half(b, a_p, hi), half(b, a_p, hi), a_prev, 6)
    out(2, a_p)
    over(b, a, 0)
    over(b, a_m, 1)
    over(b, a_p, 2)
    up2.wait_recv()
    down2.wait_recv()
    out(3, a_o)
    over(b, a_o, 3)
    far = []
    for j, (aa, u, d, slot) in enumerate(outer):
        u.wait_recv()
        u2 = copy(half(b_m, aa, lo), half(b_m, aa, lo), b_next, slot)
        over(b_m, aa, 4 + j)
        d.wait_recv()
        d2 = copy(half(b_p, aa, hi), half(b_p, aa, hi), b_prev, slot + 1)
        over(b_p, aa, 8 + j)
        far.append((aa, u2, d2))
    for j, (aa, u2, d2) in enumerate(far):
        u2.wait_recv()
        d2.wait_recv()
        over(b_o, aa, 12 + j)
    for cp in across:
        cp.wait_recv()
    for cp in started:
        cp.wait_send()


N_GATHER = 3 + 4 + 16 + 16


def gather_weights(shard):
    return pl.pallas_call(
        gather_kernel,
        out_shape=jax.ShapeDtypeStruct((2, 4, 4, 4, PAD, RANK), BF16),
        in_specs=[pl.BlockSpec(memory_space=pl.ANY)],
        out_specs=pl.BlockSpec(memory_space=pltpu.VMEM),
        scratch_shapes=[
            pltpu.SemaphoreType.DMA((N_GATHER,)),
            pltpu.SemaphoreType.DMA((N_GATHER,)),
            pltpu.SemaphoreType.DMA,
        ],
        compiler_params=pltpu.CompilerParams(
            collective_id=1, has_side_effects=True, vmem_limit_bytes=24 << 20
        ),
        name="gather_weights",
    )(shard)


def reduce_kernel(g, out, sibling, mid_p, mid_m, end_p, end_m, total, imid, iend, inner, last,
                  send, recv):
    x, yh, yl, z, c = place()
    o = 1 - c
    b = z * o + x * c
    a = x * o + z * c
    sib = device(x, yh, yl, z, o)
    a_next, a_prev = along_a(x, yh, yl, z, c, 1), along_a(x, yh, yl, z, c, 3)
    b_next, b_prev = along_b(x, yh, yl, z, c, 1), along_b(x, yh, yl, z, c, 3)
    y = yh * 2 + yl
    column = []
    for d in range(1, 4):
        yy = (y + d) % 4
        for i in range(2):
            column.append((d, yy, i, device(x, yy // 2, yy % 2, z, i)))
    meet([sib, a_next, a_prev, b_next, b_prev] + [t[3] for t in column])
    n = [0]
    started = []

    def copy(src, dst, to, slot=None):
        cp = pltpu.make_async_remote_copy(
            src_ref=src,
            dst_ref=dst,
            send_sem=send.at[n[0]],
            recv_sem=recv.at[n[0] if slot is None else slot],
            device_id=to,
            device_id_type=MESH,
        )
        n[0] += 1
        started.append(cp)
        cp.start()
        return cp

    steps = (2, 1, 3, 0)
    lo, hi = pl.ds(0, 2), pl.ds(2, 2)
    crossing = {}
    for db in steps:
        for da in steps:
            bb, aa = (a + db) % 4, (b + da) % 4
            crossing[db, da] = copy(g.at[o, bb, aa], sibling.at[bb, aa], sib)
    got = set()

    def mine(db, da, h):
        if (db, da) not in got:
            crossing[db, da].wait_recv()
            got.add((db, da))
        bb, aa = (b + db) % 4, (a + da) % 4
        return g[c, bb, aa, h].astype(F32) + sibling[bb, aa, h].astype(F32)

    def keep(db, da, h, value):
        sibling[(b + db) % 4, (a + da) % 4, h] = value.astype(BF16)

    def at(db, da, h):
        return sibling.at[(b + db) % 4, (a + da) % 4, h]

    all_k = pl.ds(0, 4)
    first = {}
    for j, da in enumerate(steps):
        keep(2, da, all_k, mine(2, da, all_k))
        first[da] = (
            copy(at(2, da, lo), mid_p.at[j], b_next),
            copy(at(2, da, hi), mid_m.at[j], b_prev),
        )
    second = {}
    for j, da in enumerate(steps):
        p, m = first[da]
        keep(1, da, hi, mine(1, da, hi))
        keep(3, da, lo, mine(3, da, lo))
        p.wait_recv()
        keep(1, da, lo, mine(1, da, lo) + mid_p[j].astype(F32))
        sp = copy(at(1, da, all_k), end_p.at[j], b_next)
        m.wait_recv()
        keep(3, da, hi, mine(3, da, hi) + mid_m[j].astype(F32))
        sm = copy(at(3, da, all_k), end_m.at[j], b_prev)
        second[da] = (sp, sm)

    def summed(j, da):
        p, m = second[da]
        own = mine(0, da, all_k)
        p.wait_recv()
        own = own + end_p[j].astype(F32)
        m.wait_recv()
        return own + end_m[j].astype(F32)

    total[0] = summed(0, 2).astype(BF16)
    fp = copy(total.at[0, lo], imid.at[0], a_next)
    fm = copy(total.at[0, hi], imid.at[1], a_prev)
    near_p = summed(1, 1)
    near_m = summed(2, 3)
    total[1, hi] = near_p[2:4].astype(BF16)
    total[2, lo] = near_m[0:2].astype(BF16)
    fp.wait_recv()
    total[1, lo] = (near_p[0:2] + imid[0].astype(F32)).astype(BF16)
    gp = copy(total.at[1], iend.at[0], a_next)
    fm.wait_recv()
    total[2, hi] = (near_m[2:4] + imid[1].astype(F32)).astype(BF16)
    gm = copy(total.at[2], iend.at[1], a_prev)
    own = summed(3, 0)
    gp.wait_recv()
    own = own + iend[0].astype(F32)
    gm.wait_recv()
    own = own + iend[1].astype(F32)
    inner[...] = own.astype(BF16)
    base = n[0]
    for d, yy, i, to in column:
        copy(inner.at[(yy // 2) * 2 + i], last.at[d, c], to, base + 2 * (d - 1) + c)
    copy(inner.at[yh * 2 + o], last.at[0, c], sib).wait_recv()
    ready = inner[yh * 2 + c].astype(F32)
    for d in range(1, 4):
        for i in range(2):
            pltpu.make_async_remote_copy(
                src_ref=inner.at[0],
                dst_ref=last.at[d, i],
                send_sem=send.at[0],
                recv_sem=recv.at[base + 2 * (d - 1) + i],
                device_id=sib,
                device_id_type=MESH,
            ).wait_recv()
    for i in range(2):
        far = last[1, i].astype(F32) + last[2, i].astype(F32) + last[3, i].astype(F32)
        near = jnp.where(c == i, ready, last[0, i].astype(F32))
        out[i] = far + near
    for cp in started:
        cp.wait_send()


N_REDUCE = 16 + 8 + 8 + 4 + 7


def reduce_gradients(g):
    half = (2, PAD, RANK)
    whole = (4, PAD, RANK)
    return pl.pallas_call(
        reduce_kernel,
        out_shape=jax.ShapeDtypeStruct((2, PAD, RANK), F32),
        in_specs=[pl.BlockSpec(memory_space=pltpu.VMEM)],
        out_specs=pl.BlockSpec(memory_space=pltpu.VMEM),
        scratch_shapes=[
            pltpu.VMEM((4, 4) + whole, BF16),
            pltpu.VMEM((4,) + half, BF16),
            pltpu.VMEM((4,) + half, BF16),
            pltpu.VMEM((4,) + whole, BF16),
            pltpu.VMEM((4,) + whole, BF16),
            pltpu.VMEM((3,) + whole, BF16),
            pltpu.VMEM((2,) + half, BF16),
            pltpu.VMEM((2,) + whole, BF16),
            pltpu.VMEM(whole, BF16),
            pltpu.VMEM((4, 2, PAD, RANK), BF16),
            pltpu.SemaphoreType.DMA((N_REDUCE,)),
            pltpu.SemaphoreType.DMA((N_REDUCE,)),
        ],
        compiler_params=pltpu.CompilerParams(
            collective_id=2, has_side_effects=True, vmem_limit_bytes=40 << 20
        ),
        name="reduce_gradients",
    )(g)


def shard_of(m, w):
    x, yh, z, c = w // 16, (w // 8) % 2, (w // 2) % 4, w % 2
    return (m, z, x, yh * 2 + c) if m == 0 else (m, x, z, yh * 2 + c)


def backward_kernel(slots, full, stacked, upstream, counts, v, u, bias, dense, slot_grad, g,
                    pg, gv, gu, gb):
    for w in range(64):
        rows = slice(ROWS * w, ROWS * (w + 1))
        v[rows, :] = full[shard_of(0, w)][0:ROWS]
        u[rows, :] = full[shard_of(1, w)][0:ROWS]
        bias[0:1, rows] = full[shard_of(0, w)][ROWS : ROWS + 1, 0:ROWS].astype(F32)
    low = jnp.zeros((SAMP, RANK), F32)
    lg = jnp.zeros((SAMP, RANK), F32)
    for j in range(WIDTH // BLK):
        cols = slice(BLK * j, BLK * (j + 1))
        st = stacked[:, cols]
        scale = upstream[:, cols].astype(F32) * st.astype(F32)
        gb[0:1, cols] = jnp.sum(scale, axis=0, keepdims=True)
        p = scale.astype(BF16)
        pg[:, cols] = p
        low = low + jnp.dot(st, v[cols, :], preferred_element_type=F32)
        lg = lg + jnp.dot(p, u[cols, :], preferred_element_type=F32)
    low = low.astype(BF16)
    lg = lg.astype(BF16)
    slot_grad[...] = jnp.zeros_like(slot_grad)
    inverse = 1.0 / counts[...].astype(F32)
    for j in range(WIDTH // BLK):
        cols = slice(BLK * j, BLK * (j + 1))
        up = upstream[:, cols].astype(F32)
        projected = lax.dot_general(low, u[cols, :], OVER_COLS, preferred_element_type=F32)
        through = lax.dot_general(lg, v[cols, :], OVER_COLS, preferred_element_type=F32)
        grad = up * (projected + bias[0:1, cols]) + up + through
        for i in range(BLK // E):
            t = j * (BLK // E) + i - 1
            piece = grad[:, E * i : E * (i + 1)]
            if t < 0:
                dense[...] = piece.astype(BF16)
            else:
                slot_grad[slots[t]] = (piece * inverse[:, t : t + 1]).astype(BF16)
        gu[cols, :] = lax.dot_general(
            pg[:, cols], low, OVER_ROWS, preferred_element_type=F32
        ).astype(BF16)
        gv[cols, :] = lax.dot_general(
            stacked[:, cols], lg, OVER_ROWS, preferred_element_type=F32
        ).astype(BF16)
    for w in range(64):
        rows = slice(ROWS * w, ROWS * (w + 1))
        g[shard_of(0, w) + (slice(0, ROWS),)] = gv[rows, :]
        g[shard_of(1, w) + (slice(0, ROWS),)] = gu[rows, :]
        g[shard_of(0, w) + (slice(ROWS, ROWS + 1), slice(0, ROWS))] = gb[0:1, rows].astype(BF16)


def backward(full, stacked, upstream, counts, slots):
    vmem = pl.BlockSpec(memory_space=pltpu.VMEM)
    return pl.pallas_call(
        backward_kernel,
        out_shape=(
            jax.ShapeDtypeStruct((WIDTH, RANK), BF16),
            jax.ShapeDtypeStruct((WIDTH, RANK), BF16),
            jax.ShapeDtypeStruct((1, WIDTH), F32),
            jax.ShapeDtypeStruct((SAMP, E), BF16),
            jax.ShapeDtypeStruct((SLOTS, SAMP, E), BF16),
            jax.ShapeDtypeStruct((2, 4, 4, 4, PAD, RANK), BF16),
        ),
        in_specs=[pl.BlockSpec(memory_space=pltpu.SMEM)] + [vmem] * 4,
        out_specs=[vmem] * 6,
        scratch_shapes=[
            pltpu.VMEM((SAMP, WIDTH), BF16),
            pltpu.VMEM((WIDTH, RANK), BF16),
            pltpu.VMEM((WIDTH, RANK), BF16),
            pltpu.VMEM((1, WIDTH), F32),
        ],
        compiler_params=pltpu.CompilerParams(vmem_limit_bytes=60 << 20),
        cost_estimate=pl.CostEstimate(
            flops=6 * 2 * SAMP * WIDTH * RANK, bytes_accessed=40 << 20, transcendentals=0
        ),
        name="backward_a",
    )(slots, full, stacked, upstream, counts)


def forward_kernel(slots, arrived, dense, counts, v, u, bias, crossed, st):
    inverse = 1.0 / counts[...].astype(F32)
    st[:, 0:E] = dense[...]
    for t in range(TABLES):
        mean = arrived[slots[t]].astype(F32) * inverse[:, t : t + 1]
        st[:, E * (t + 1) : E * (t + 2)] = mean.astype(BF16)
    low = jnp.zeros((SAMP, RANK), F32)
    for j in range(WIDTH // BLK):
        cols = slice(BLK * j, BLK * (j + 1))
        low = low + jnp.dot(st[:, cols], v[cols, :], preferred_element_type=F32)
    low = low.astype(BF16)
    for j in range(WIDTH // BLK):
        cols = slice(BLK * j, BLK * (j + 1))
        wide = st[:, cols].astype(F32)
        projected = lax.dot_general(low, u[cols, :], OVER_COLS, preferred_element_type=F32)
        crossed[:, cols] = (wide * (projected + bias[0:1, cols]) + wide).astype(BF16)


def forward(arrived, dense, counts, slots, v, u, bias):
    vmem = pl.BlockSpec(memory_space=pltpu.VMEM)
    return pl.pallas_call(
        forward_kernel,
        out_shape=jax.ShapeDtypeStruct((SAMP, WIDTH), BF16),
        in_specs=[pl.BlockSpec(memory_space=pltpu.SMEM)] + [vmem] * 6,
        out_specs=vmem,
        scratch_shapes=[pltpu.VMEM((SAMP, WIDTH), BF16)],
        compiler_params=pltpu.CompilerParams(vmem_limit_bytes=40 << 20),
        cost_estimate=pl.CostEstimate(
            flops=2 * 2 * SAMP * WIDTH * RANK, bytes_accessed=16 << 20, transcendentals=0
        ),
        name="forward_b",
    )(slots, arrived, dense, counts, v, u, bias)


def local(
    pooled_b,
    dense_output_second,
    counts_b,
    slot_of,
    stacked_a,
    upstream_a,
    counts_a,
    down_projection,
    proj_up,
    cross_layer_bias,
):
    slots = slot_of[:TABLES]
    arrived = lax.all_to_all(pooled_b, "wide", split_axis=1, concat_axis=0, tiled=True)
    bias_row = jnp.pad(cross_layer_bias[None, :], ((0, 1), (0, RANK - ROWS)))
    shard = jnp.stack(
        [
            jnp.concatenate([down_projection, bias_row], axis=0),
            jnp.pad(jnp.transpose(proj_up), ((0, PAD - ROWS), (0, 0))),
        ]
    )
    full = gather_weights(shard)
    v, u, bias, dense_gradient, slot_grad, g = backward(
        full, stacked_a, upstream_a, counts_a, slots
    )
    returned = lax.all_to_all(
        slot_grad.reshape(SLOTS, 1, SAMP, E), "wide", split_axis=0, concat_axis=1, tiled=True
    )
    sums = reduce_gradients(g)
    crossed_b = forward(
        arrived.reshape(SLOTS, SAMP, E), dense_output_second, counts_b, slots, v, u, bias
    )
    return (
        crossed_b,
        dense_gradient,
        returned,
        sums[0, :ROWS],
        jnp.transpose(sums[1, :ROWS]),
        sums[0, ROWS, :ROWS],
    )


def solution(mesh):
    return jax.shard_map(
        local,
        mesh=mesh,
        in_specs=(
            P("wide", None, "pair", None),
            P(("wide", "pair"), None),
            P(("wide", "pair"), None),
            P(),
            P(("wide", "pair"), None),
            P(("wide", "pair"), None),
            P(("wide", "pair"), None),
            P("wide", None),
            P(None, "wide"),
            P("wide"),
        ),
        out_specs=(
            P(("wide", "pair"), None),
            P(("wide", "pair"), None),
            P("wide", None, "pair", None),
            P("wide", None),
            P(None, "wide"),
            P("wide"),
        ),
        check_vma=False,
    )
```

time: 376 us -> 219 us (0.58)
  Pallas kernels: 0 us -> 136 us
  waiting for transfers between devices: 109 us -> 0.01 us
  blocking collectives: 140 us -> 59.3 us
  local copies, waits for them, and re-layouts: 50.8 us -> 16 us
  matrix products: 25.4 us -> 0 us
  other arithmetic: 15.4 us -> 0.89 us
  between operations: 14.2 us -> 0.71 us
  starting transfers between devices: 19 us -> 5.72 us
    unnamed x1 -> x0, blocking collectives: 137 us -> none
    pallas_call x0 -> x4, Pallas kernels: none -> 136 us  [the longest x1 74.5 us: reduce_gradients(): pl.pallas_call(reduce_kernel, out_shape=jax.ShapeDtypeStruct((2, PAD, RAN...]
    all_gather x1 -> x0, waiting for transfers between devices: 109 us -> none  [gather_turned(): filled = lax.all_gather(both, axis, axis=0, tiled=True)]
    all_to_all x0 -> x1, blocking collectives: none -> 59.3 us  [local(): lax.all_to_all(slot_grad.reshape(SLOTS, 1, SAMP, E), 'wide', split_axis=0...]
    dot_general x8 -> x0, matrix products: 25.4 us -> none  [the longest x2 7.78 us: cross_forward(): projected = jnp.dot(low_rank, up, preferred_element_type=jnp.float32)]
    convert_element_type x3 -> x0, local copies, waits for them, and re-layouts: 12 us -> none  [the longest x2 7.54 us: table_means(): jnp.transpose(scaled, (1, 0, 2)).reshape(scaled.shape[1], -1)]
    convert_element_type x7 -> x0, other arithmetic: 11.6 us -> none  [the longest x1 3.57 us: cross_backward(): jnp.transpose(table_gradient, (1, 0, 2)).astype(jnp.bfloat16)]
    slice x3 -> x0, local copies, waits for them, and re-layouts: 8.51 us -> none  [the longest x2 6.97 us: cross_backward(): input_grad[:, feature_index:].reshape(rows, -1, feature_index)]
  transfers between devices with their start and end apart: 3 -> 1, of which waited for: 1 -> 0; matrix products, arithmetic and copies ran while one was open for 22% -> 1% of each run, Pallas kernels for 0% -> 34%
where the time goes in v1:
time: 219 us
  Pallas kernels  136 us (62%)
  blocking collectives  59.3 us (27%)
  local copies, waits for them, and re-layouts  16 us (7%)
  starting transfers between devices  5.72 us (3%)
    pallas_call x1, Pallas kernels, reduce_gradients(): pl.pallas_call(reduce_kernel, out_shape=jax.ShapeDtypeStruct((2, PAD, RAN...  74.5 us
    all_to_all x1, blocking collectives, local(): lax.all_to_all(slot_grad.reshape(SLOTS, 1, SAMP, E), 'wide', split_axis=0...  59.3 us
    pallas_call x1, Pallas kernels, gather_weights(): pl.pallas_call(gather_kernel, out_shape=jax.ShapeDtypeStruct((2, 4, 4, 4,...  36.6 us
    pallas_call x1, Pallas kernels, backward(): pl.pallas_call(backward_kernel, out_shape=(jax.ShapeDtypeStruct((WIDTH, R...  18.6 us
    unnamed x23, local copies, waits for them, and re-layouts  14.8 us
    pallas_call x1, Pallas kernels, forward(): pl.pallas_call(forward_kernel, out_shape=jax.ShapeDtypeStruct((SAMP, WIDT...  6.35 us
    all_to_all x1, starting transfers between devices, local(): lax.all_to_all(pooled_b, 'wide', split_axis=1, concat_axis=0, tiled=True)  5.72 us
  transfers between devices with their start and end apart: 1, of which 0 were waited for; matrix products, arithmetic and copies ran while one was open for 1% of the time, Pallas kernels for 34%

profile of v1, /device:TPU:1, one launch (start us, length us, event | category | flops | bytes accessed | tf_op | source)
XLA Modules:
  0.0 218.7 jit_solution(13727096255829933538)
XLA Ops:
  0.6 0.0 copy-start.9
  0.6 0.9 fusion.2
  1.5 36.6 %gather_weights.1.full = bf16[2,4,4,4,56,512]{5,4,3,2,1,0:T(8,128)(2,1)S(1)} custom-call(bf16[2,56,512]{2,1,0:T(8,128)(2,1)S(1)} %pad_maximum_fusion.shard), custom_call_target="tpu_custom_call" | custom-call | tf_op jit(solution)/shard_map/gather_weights/pallas_call | solution.py:157
  38.2 0.0 copy-start
  38.2 3.0 %copy-done = bf16[2,4,4,4,56,512]{5,4,3,2,1,0:T(8,128)(2,1)} copy-done((bf16[2,4,4,4,56,512]{5,4,3,2,1,0:T(8,128)(2,1)}, bf16[2,4,4,4,56,512]{5,4,3,2,1,0:T(8,128)(2,1)S(1)}, u32[]{:S(2)}) %copy-start) | copy-done | bytes 7340056
  41.2 0.0 copy-done.9
  41.2 0.8 copy.19.counts
  42.0 18.6 %backward_a.1 = (bf16[3456,512]{1,0:T(8,128)(2,1)}, bf16[3456,512]{1,0:T(8,128)(2,1)}, f32[1,3456]{1,0:T(1,128)}, bf16[256,128]{1,0:T(8,128)(2,1)}, bf16[64,256,...) custom-call(s32[26]{0:T(128)} %bitcast.21, bf16[2,4,4,4,56,512]{5,4,3,2,1,0:T(8,128)(2,1)} %copy-done, ...), custom_call_target="tpu_custom_call" | custom-call | flops 5435817984 | bytes 41943040 | tf_op jit(solution)/shard_map/backward_a/pallas_call | solution.py:387
  60.6 59.3 %all_to_all.21 = bf16[64,1,256,128]{3,2,1,0:T(8,128)(2,1)} all-to-all(bf16[64,1,256,128]{3,2,1,0:T(8,128)(2,1)} %bitcast.25), channel_id=1, replica_groups=mesh['wide'=64,'pair'=2] {'wide'}, dimensions={0} | all-to-all | bytes 8388608 | tf_op jit(solution)/shard_map/all_to_all | solution.py:472
  119.8 5.7 %all-to-all-start = ((bf16[1,64,256,128]{3,2,0,1:T(8,128)(2,1)}), bf16[1,64,256,128]{3,2,0,1:T(8,128)(2,1)}, u32[]{:S(2)}, u32[]{:S(2)}) async-start(bf16[1,64,256,128]{3,2,0,1:T(8,128)(2,1)} %bitcast.24), calls=%async_computation | async-start | bytes 8388608 | tf_op jit(solution)/shard_map/all_to_all | solution.py:460
  125.6 0.0 copy-start.6
  125.6 1.5 copy.20.counts
  127.1 3.1 %copy-done.1 = bf16[2,4,4,4,56,512]{5,4,3,2,1,0:T(8,128)(2,1)S(1)} copy-done((bf16[2,4,4,4,56,512]{5,4,3,2,1,0:T(8,128)(2,1)S(1)}, bf16[2,4,4,4,56,512]{5,4,3,2,1,0:T(8,128)(2,1)}, u32[]{:S(2)}) %copy-start.1) | copy-done | bytes 7340056
  130.2 74.5 %reduce_gradients.1 = f32[2,56,512]{2,1,0:T(8,128)S(1)} custom-call(bf16[2,4,4,4,56,512]{5,4,3,2,1,0:T(8,128)(2,1)S(1)} %copy-done.1), custom_call_target="tpu_custom_call" | custom-call | tf_op jit(solution)/shard_map/reduce_gradients/pallas_call | solution.py:306
  204.7 0.5 slice_bitcast_fusion.2
  205.2 0.7 slice_bitcast_fusion
  205.9 0.0 all-to-all-done
  205.9 0.0 copy-done.2
  205.9 2.0 copy-done.3
  207.9 0.9 copy-done.4
  208.8 0.8 copy-done.5
  209.6 0.7 copy-done.7
  210.3 6.4 %forward_b.1 = bf16[256,3456]{1,0:T(8,128)(2,1)} custom-call(s32[26]{0:T(128)S(1)} %bitcast.22, bf16[64,256,128]{2,1,0:T(8,128)(2,1)} %bitcast.1.arrived, bf16[256,128]{1,0:T(8,128)(2,1)S(1)} %copy-done.5, s32[256,26]{1,0:T(8,128)S(1)} %copy-done.4, bf16[3456,512]{1,0:T(8,128)(2,1)S(1)} %copy-done.2, bf16[3456,512]{1,0:T(8,128)(2,1)S(1)} %copy-done.3, ...), custom_call_target="tpu_custom_call" | custom-call | flops 1811939328 | bytes 16777216 | tf_op jit(solution)/shard_map/forward_b/pallas_call | solution.py:433
  216.6 2.0 copy.23
  (10 shorter events, 0.0 us)
Async XLA Ops:
  0.6 40.6 %copy-start.9 = (s32[256,26]{0,1:T(8,128)S(1)}, s32[256,26]{0,1:T(8,128)}, u32[]{:S(2)}) copy-start(s32[256,26]{0,1:T(8,128)} %param.16) | copy-start | bytes 79876
  38.2 3.0 %copy-start = (bf16[2,4,4,4,56,512]{5,4,3,2,1,0:T(8,128)(2,1)}, bf16[2,4,4,4,56,512]{5,4,3,2,1,0:T(8,128)(2,1)S(1)}, u32[]{:S(2)}) copy-start(bf16[2,4,4,4,56,512]{5,4,3,2,1,0:T(8,128)(2,1)S(1)} %gather_weights.1.full) | copy-start | bytes 22020100
  119.8 86.0 %copy-start.2 = (bf16[3456,512]{1,0:T(8,128)(2,1)S(1)}, bf16[3456,512]{1,0:T(8,128)(2,1)}, u32[]{:S(2)}) copy-start(bf16[3456,512]{1,0:T(8,128)(2,1)} %get-tuple-element.12.v) | copy-start | bytes 10616836
  119.8 86.0 %all-to-all-start = ((bf16[1,64,256,128]{3,2,0,1:T(8,128)(2,1)}), bf16[1,64,256,128]{3,2,0,1:T(8,128)(2,1)}, u32[]{:S(2)}, u32[]{:S(2)}) async-start(bf16[1,64,256,128]{3,2,0,1:T(8,128)(2,1)} %bitcast.24), calls=%async_computation | async-start | bytes 8388608 | tf_op jit(solution)/shard_map/all_to_all | solution.py:460
  125.6 80.3 %copy-start.6 = (f32[1,3456]{1,0:T(1,128)S(1)}, f32[1,3456]{1,0:T(1,128)}, u32[]{:S(2)}) copy-start(f32[1,3456]{1,0:T(1,128)} %get-tuple-element.14.bias) | copy-start | bytes 41476
  127.1 3.1 %copy-start.1 = (bf16[2,4,4,4,56,512]{5,4,3,2,1,0:T(8,128)(2,1)S(1)}, bf16[2,4,4,4,56,512]{5,4,3,2,1,0:T(8,128)(2,1)}, u32[]{:S(2)}) copy-start(bf16[2,4,4,4,56,512]{5,4,3,2,1,0:T(8,128)(2,1)} %get-tuple-element.17.g) | copy-start | bytes 22020100
  205.9 2.0 copy-start.3
  207.9 0.9 copy-start.4
  208.8 0.8 copy-start.5
  209.6 0.7 copy-start.7
  210.3 6.4 %copy-start.8 = (bf16[64,1,256,128]{3,2,1,0:T(8,128)(2,1)S(1)}, bf16[64,1,256,128]{3,2,1,0:T(8,128)(2,1)}, u32[]{:S(2)}) copy-start(bf16[64,1,256,128]{3,2,1,0:T(8,128)(2,1)} %all_to_all.21) | copy-start | bytes 12582916

commit v2 on v1

v2 whole, which is shorter than its diff:
```python
import itertools

import jax
import jax.numpy as jnp
from jax import lax
from jax.experimental import pallas as pl
from jax.experimental.pallas import tpu as pltpu
from jax.sharding import PartitionSpec as P

MESH = pl.DeviceIdType.MESH
F32 = jnp.float32
BF16 = jnp.bfloat16

ROWS = 54
PAD = 56
RANK = 512
E = 128
TABLES = 26
SLOTS = 64
SAMP = 256
WIDTH = 3456
BLK = 384
OVER_ROWS = (((0,), (0,)), ((), ()))
OVER_COLS = (((1,), (1,)), ((), ()))


def place():
    w = lax.axis_index("wide")
    yl = lax.axis_index("pair")
    return w // 16, (w // 8) % 2, yl, (w // 2) % 4, w % 2


def device(x, yh, yl, z, c):
    return (((x * 2 + yh) * 4 + z) * 2 + c, yl)


def along_a(x, yh, yl, z, c, d):
    return device((x + d * (1 - c)) % 4, yh, yl, (z + d * c) % 4, c)


def along_b(x, yh, yl, z, c, d):
    return device((x + d * c) % 4, yh, yl, (z + d * (1 - c)) % 4, c)


def load_of(offset):
    dx, dy, dz, _ = offset
    loads = [0] * 6
    for d, at in ((dx, 0), (dz, 2)):
        if d % 2:
            loads[at + (d == 3)] += 1
        elif d:
            loads[at] += 1
            loads[at + 1] += 1
    if dy:
        loads[4] += 1
        loads[5] += 1
    return loads


def exchange_order():
    left = [o for o in itertools.product(range(4), range(2), range(4), range(2)) if any(o)]
    total, order = [0] * 6, []
    while left:

        def cost(offset):
            after = [p + q for p, q in zip(total, load_of(offset))]
            return max(after) - min(after), -sum(load_of(offset))

        best = min(left, key=cost)
        left.remove(best)
        order.append(best)
        total = [p + q for p, q in zip(total, load_of(best))]
    return order


ORDER = exchange_order()
N_GATHER = 3 + 4 + 16 + 16
N_REDUCE = 16 + 8 + 8 + 4 + 7
FEED_B = (0, 4, 4, 4, 4, 4, 4, 4, 4)
FEED_A = (8, 4, 4, 4, 4, 4, 4, 4, 4, 4)


def target(me, offset):
    x, yh, _, z, c = me
    dx, dy, dz, dc = offset
    sx = dx + ((4 - dx) % 4 - dx) * c
    sz = dz + ((4 - dz) % 4 - dz) * c
    return ((((x + sx) % 4) * 2 + (yh + dy) % 2) * 4 + (z + sz) % 4) * 2 + (c + dc) % 2


def shard_of(m, w):
    x, yh, z, c = w // 16, (w // 8) % 2, (w // 2) % 4, w % 2
    return (m, z, x, yh * 2 + c) if m == 0 else (m, x, z, yh * 2 + c)


def step_kernel(slots, index, pooled, shard, stacked_h, upstream_h, counts_a_h, dense_h, counts_b_h,
                crossed_h, dense_g, returned, out,
                full, v, u, bias, stacked, upstream, pg, gv, gu, gb, tg, snd, arrived, st, counts_a,
                counts_b, sibling, mid_p, mid_m, end_p, end_m, total, imid, iend, inner, last,
                gsend, grecv, rsend, rrecv, local_sem, bsend, brecv, asend, arecv):
    place_of = place()
    x, yh, yl, z, c = place_of
    me = lax.axis_index("wide")
    o = 1 - c
    b = z * o + x * c
    a = x * o + z * c
    k = yh * 2 + c
    y = yh * 2 + yl
    sib = device(x, yh, yl, z, o)
    part = [device(x, 1 - yh, 1 - yl, z, i) for i in range(2)]
    a_next, a_prev = along_a(x, yh, yl, z, c, 1), along_a(x, yh, yl, z, c, 3)
    b_next, b_prev = along_b(x, yh, yl, z, c, 1), along_b(x, yh, yl, z, c, 3)
    lo, hi, all_k = pl.ds(0, 2), pl.ds(2, 2), pl.ds(0, 4)

    def load(src, dst, i):
        cp = pltpu.make_async_copy(src, dst, local_sem.at[i])
        cp.start()
        return cp

    loads = [
        load(stacked_h, stacked, 0),
        load(upstream_h, upstream, 1),
        load(counts_a_h, counts_a, 2),
        load(counts_b_h, counts_b, 3),
        load(dense_h, st.at[:, pl.ds(0, E)], 4),
    ]
    mine_b = load(pooled.at[me], arrived.at[me], 5)
    mine_w = load(shard.at[c], full.at[c, b, a, k], 6)

    barrier = pltpu.get_barrier_semaphore()

    @pl.loop(0, SLOTS)
    def _(i):
        @pl.when(i != me)
        def _():
            pl.semaphore_signal(barrier, inc=1, device_id=(i, yl), device_id_type=MESH)

    for d in (1, 3):
        for i in range(2):
            yy = (y + d) % 4
            pl.semaphore_signal(
                barrier, inc=1, device_id=device(x, yy // 2, yy % 2, z, i), device_id_type=MESH
            )
    pl.semaphore_wait(barrier, SLOTS - 1 + 4)

    fed = [0, 0]

    def feed_b(count):
        for offset in ORDER[fed[0] : fed[0] + count]:
            to = target(place_of, offset)
            pltpu.make_async_remote_copy(
                src_ref=pooled.at[to],
                dst_ref=arrived.at[me],
                send_sem=bsend,
                recv_sem=brecv,
                device_id=(to, yl),
                device_id_type=MESH,
            ).start()
        fed[0] += count

    def feed_a(count):
        for offset in ORDER[fed[1] : fed[1] + count]:
            to = target(place_of, offset)
            pltpu.make_async_remote_copy(
                src_ref=snd.at[to],
                dst_ref=returned.at[me],
                send_sem=asend,
                recv_sem=arecv,
                device_id=(to, yl),
                device_id_type=MESH,
            ).start()
        fed[1] += count

    n = [0]
    started = []

    def gcopy(src, dst, to, slot):
        cp = pltpu.make_async_remote_copy(
            src_ref=src,
            dst_ref=dst,
            send_sem=gsend.at[n[0]],
            recv_sem=grecv.at[slot],
            device_id=to,
            device_id_type=MESH,
        )
        n[0] += 1
        started.append(cp)
        cp.start()
        return cp

    s1 = []
    for i in range(2):
        bi, ai = (z, x) if i == 0 else (x, z)
        s1.append(gcopy(shard.at[i], full.at[i, bi, ai, k], part[i], 1 + (c + i) % 2))
    s1.append(gcopy(shard.at[o], full.at[o, a, b, k], sib, 0))
    feed_b(FEED_B[0])
    mine_w.wait()
    for cp in s1:
        cp.wait_recv()
    a_m, a_p, a_o = (a + 3) % 4, (a + 1) % 4, (a + 2) % 4
    b_m, b_p, b_o = (b + 3) % 4, (b + 1) % 4, (b + 2) % 4

    def ring(at, aa, to, slot, h=all_k):
        return gcopy(full.at[c, at, aa, h], full.at[c, at, aa, h], to, slot)

    outer = []

    def out_ring(j, aa):
        nxt = ring(b, aa, b_next, 7 + 4 * j)
        prv = ring(b, aa, b_prev, 8 + 4 * j)
        outer.append((aa, nxt, prv, 9 + 4 * j))

    across = []

    def over(bb, aa, j):
        across.append(ring(bb, aa, sib, 23 + j))

    up = ring(b, a, a_next, 3)
    down = ring(b, a, a_prev, 4)
    out_ring(0, a)
    feed_b(FEED_B[1])
    up.wait_recv()
    up2 = ring(b, a_m, a_next, 5, lo)
    out_ring(1, a_m)
    down.wait_recv()
    down2 = ring(b, a_p, a_prev, 6, hi)
    out_ring(2, a_p)
    over(b, a, 0)
    over(b, a_m, 1)
    over(b, a_p, 2)
    feed_b(FEED_B[2])
    up2.wait_recv()
    down2.wait_recv()
    out_ring(3, a_o)
    over(b, a_o, 3)
    feed_b(FEED_B[3])
    far = []
    for j, (aa, nxt, prv, slot) in enumerate(outer):
        nxt.wait_recv()
        n2 = ring(b_m, aa, b_next, slot, lo)
        over(b_m, aa, 4 + j)
        prv.wait_recv()
        p2 = ring(b_p, aa, b_prev, slot + 1, hi)
        over(b_p, aa, 8 + j)
        far.append((aa, n2, p2))
        feed_b(FEED_B[4 + j])
    for j, (aa, n2, p2) in enumerate(far):
        n2.wait_recv()
        p2.wait_recv()
        over(b_o, aa, 12 + j)
    feed_b(FEED_B[8])
    for cp in across:
        cp.wait_recv()
    for cp in started:
        cp.wait_send()
    feed_b(len(ORDER) - fed[0])

    for cp in loads[:3]:
        cp.wait()
    for w in range(64):
        rows = slice(ROWS * w, ROWS * (w + 1))
        v[rows, :] = full[shard_of(0, w)][0:ROWS]
        u[rows, :] = full[shard_of(1, w)][0:ROWS]
        bias[0:1, rows] = full[shard_of(0, w)][ROWS : ROWS + 1, 0:ROWS].astype(F32)
    low = jnp.zeros((SAMP, RANK), F32)
    lg = jnp.zeros((SAMP, RANK), F32)
    for j in range(WIDTH // BLK):
        cols = slice(BLK * j, BLK * (j + 1))
        sa = stacked[:, cols]
        scale = upstream[:, cols].astype(F32) * sa.astype(F32)
        gb[0:1, cols] = jnp.sum(scale, axis=0, keepdims=True)
        p = scale.astype(BF16)
        pg[:, cols] = p
        low = low + jnp.dot(sa, v[cols, :], preferred_element_type=F32)
        lg = lg + jnp.dot(p, u[cols, :], preferred_element_type=F32)
    low = low.astype(BF16)
    lg = lg.astype(BF16)
    tg[0] = jnp.zeros((SAMP, E), BF16)
    inverse = (1.0 / counts_a[...].astype(F32)).T
    for j in range(WIDTH // BLK):
        cols = slice(BLK * j, BLK * (j + 1))
        ua = upstream[:, cols].astype(F32)
        projected = lax.dot_general(low, u[cols, :], OVER_COLS, preferred_element_type=F32)
        through = lax.dot_general(lg, v[cols, :], OVER_COLS, preferred_element_type=F32)
        grad = ua * (projected + bias[0:1, cols]) + ua + through
        for i in range(BLK // E):
            t = j * (BLK // E) + i
            piece = grad[:, E * i : E * (i + 1)]
            if t == 0:
                dense_g[...] = piece.astype(BF16)
            else:
                tg[t] = (piece * inverse[:, t - 1 : t]).astype(BF16)
        gu[cols, :] = lax.dot_general(
            pg[:, cols], low, OVER_ROWS, preferred_element_type=F32
        ).astype(BF16)
        gv[cols, :] = lax.dot_general(
            stacked[:, cols], lg, OVER_ROWS, preferred_element_type=F32
        ).astype(BF16)
    for w in range(64):
        rows = slice(ROWS * w, ROWS * (w + 1))
        full[shard_of(0, w) + (slice(0, ROWS),)] = gv[rows, :]
        full[shard_of(1, w) + (slice(0, ROWS),)] = gu[rows, :]
        full[shard_of(0, w) + (slice(ROWS, ROWS + 1), slice(0, ROWS))] = gb[0:1, rows].astype(BF16)

    m = [0]
    sent = []

    def rcopy(src, dst, to, slot=None):
        cp = pltpu.make_async_remote_copy(
            src_ref=src,
            dst_ref=dst,
            send_sem=rsend.at[m[0]],
            recv_sem=rrecv.at[m[0] if slot is None else slot],
            device_id=to,
            device_id_type=MESH,
        )
        m[0] += 1
        sent.append(cp)
        cp.start()
        return cp

    steps = (2, 1, 3, 0)
    crossing = {}
    for db in steps:
        for da in steps:
            bb, aa = (a + db) % 4, (b + da) % 4
            crossing[db, da] = rcopy(full.at[o, bb, aa], sibling.at[bb, aa], sib)

    for s in range(SLOTS):
        snd[s] = tg[index[s]]
    got = set()

    def mine(db, da, h):
        if (db, da) not in got:
            crossing[db, da].wait_recv()
            got.add((db, da))
        bb, aa = (b + db) % 4, (a + da) % 4
        return full[c, bb, aa, h].astype(F32) + sibling[bb, aa, h].astype(F32)

    def keep(db, da, h, value):
        sibling[(b + db) % 4, (a + da) % 4, h] = value.astype(BF16)

    def at(db, da, h):
        return sibling.at[(b + db) % 4, (a + da) % 4, h]

    first = {}
    for j, da in enumerate(steps):
        keep(2, da, all_k, mine(2, da, all_k))
        first[da] = (
            rcopy(at(2, da, lo), mid_p.at[j], b_next),
            rcopy(at(2, da, hi), mid_m.at[j], b_prev),
        )
    home_a = load(snd.at[me], returned.at[me], 7)
    feed_a(FEED_A[0])
    second = {}
    for j, da in enumerate(steps):
        p, q = first[da]
        keep(1, da, hi, mine(1, da, hi))
        keep(3, da, lo, mine(3, da, lo))
        p.wait_recv()
        keep(1, da, lo, mine(1, da, lo) + mid_p[j].astype(F32))
        sp = rcopy(at(1, da, all_k), end_p.at[j], b_next)
        q.wait_recv()
        keep(3, da, hi, mine(3, da, hi) + mid_m[j].astype(F32))
        sm = rcopy(at(3, da, all_k), end_m.at[j], b_prev)
        second[da] = (sp, sm)
        feed_a(FEED_A[1 + j])

    def summed(j, da):
        p, q = second[da]
        own = mine(0, da, all_k)
        p.wait_recv()
        own = own + end_p[j].astype(F32)
        q.wait_recv()
        return own + end_m[j].astype(F32)

    total[0] = summed(0, 2).astype(BF16)
    fp = rcopy(total.at[0, lo], imid.at[0], a_next)
    fm = rcopy(total.at[0, hi], imid.at[1], a_prev)
    feed_a(FEED_A[5])
    near_p = summed(1, 1)
    near_m = summed(2, 3)
    total[1, hi] = near_p[2:4].astype(BF16)
    total[2, lo] = near_m[0:2].astype(BF16)
    fp.wait_recv()
    total[1, lo] = (near_p[0:2] + imid[0].astype(F32)).astype(BF16)
    gp = rcopy(total.at[1], iend.at[0], a_next)
    fm.wait_recv()
    total[2, hi] = (near_m[2:4] + imid[1].astype(F32)).astype(BF16)
    gm = rcopy(total.at[2], iend.at[1], a_prev)
    feed_a(FEED_A[6])
    own = summed(3, 0)
    gp.wait_recv()
    own = own + iend[0].astype(F32)
    gm.wait_recv()
    own = own + iend[1].astype(F32)
    inner[...] = own.astype(BF16)
    base = m[0]
    for d in range(1, 4):
        for i in range(2):
            yy = (y + d) % 4
            rcopy(
                inner.at[(yy // 2) * 2 + i],
                last.at[d, c],
                device(x, yy // 2, yy % 2, z, i),
                base + 2 * (d - 1) + c,
            )
    near = rcopy(inner.at[yh * 2 + o], last.at[0, c], sib)
    feed_a(len(ORDER) - fed[1])

    def await_exchange(send, recv, buf):
        cp = pltpu.make_async_remote_copy(
            src_ref=buf.at[pl.ds(0, SLOTS - 1)],
            dst_ref=buf.at[pl.ds(0, SLOTS - 1)],
            send_sem=send,
            recv_sem=recv,
            device_id=sib,
            device_id_type=MESH,
        )
        cp.wait_send()
        cp.wait_recv()

    for cp in loads[3:]:
        cp.wait()
    mine_b.wait()
    await_exchange(bsend, brecv, arrived)
    inverse_b = (1.0 / counts_b[...].astype(F32)).T
    for t in range(TABLES):
        mean = arrived[slots[t]].astype(F32) * inverse_b[:, t : t + 1]
        st[:, E * (t + 1) : E * (t + 2)] = mean.astype(BF16)
    low_b = jnp.zeros((SAMP, RANK), F32)
    for j in range(WIDTH // BLK):
        cols = slice(BLK * j, BLK * (j + 1))
        low_b = low_b + jnp.dot(st[:, cols], v[cols, :], preferred_element_type=F32)
    low_b = low_b.astype(BF16)
    for j in range(WIDTH // BLK):
        cols = slice(BLK * j, BLK * (j + 1))
        wide = st[:, cols].astype(F32)
        projected = lax.dot_general(low_b, u[cols, :], OVER_COLS, preferred_element_type=F32)
        st[:, cols] = (wide * (projected + bias[0:1, cols]) + wide).astype(BF16)
    write = load(st, crossed_h, 8)

    near.wait_recv()
    for d in range(1, 4):
        for i in range(2):
            pltpu.make_async_remote_copy(
                src_ref=inner.at[0],
                dst_ref=last.at[d, i],
                send_sem=rsend.at[0],
                recv_sem=rrecv.at[base + 2 * (d - 1) + i],
                device_id=sib,
                device_id_type=MESH,
            ).wait_recv()
    ready = inner[k].astype(F32)
    for i in range(2):
        others = last[1, i].astype(F32) + last[2, i].astype(F32) + last[3, i].astype(F32)
        out[i] = others + jnp.where(c == i, ready, last[0, i].astype(F32))
    for cp in sent:
        cp.wait_send()
    home_a.wait()
    write.wait()
    await_exchange(asend, arecv, returned)


def step(slots, index, pooled, shard, stacked, upstream, counts_a, dense, counts_b):
    smem = pl.BlockSpec(memory_space=pltpu.SMEM)
    vmem = pl.BlockSpec(memory_space=pltpu.VMEM)
    anywhere = pl.BlockSpec(memory_space=pl.ANY)
    half = (2, PAD, RANK)
    whole = (4, PAD, RANK)
    return pl.pallas_call(
        step_kernel,
        out_shape=(
            jax.ShapeDtypeStruct((SAMP, WIDTH), BF16),
            jax.ShapeDtypeStruct((SAMP, E), BF16),
            jax.ShapeDtypeStruct((SLOTS, SAMP, E), BF16),
            jax.ShapeDtypeStruct((2, PAD, RANK), F32),
        ),
        in_specs=[smem] * 2 + [anywhere] * 7,
        out_specs=[anywhere, vmem, anywhere, vmem],
        scratch_shapes=[
            pltpu.VMEM((2, 4, 4, 4, PAD, RANK), BF16),
            pltpu.VMEM((WIDTH, RANK), BF16),
            pltpu.VMEM((WIDTH, RANK), BF16),
            pltpu.VMEM((1, WIDTH), F32),
            pltpu.VMEM((SAMP, WIDTH), BF16),
            pltpu.VMEM((SAMP, WIDTH), BF16),
            pltpu.VMEM((SAMP, WIDTH), BF16),
            pltpu.VMEM((WIDTH, RANK), BF16),
            pltpu.VMEM((WIDTH, RANK), BF16),
            pltpu.VMEM((1, WIDTH), F32),
            pltpu.VMEM((TABLES + 1, SAMP, E), BF16),
            pltpu.VMEM((SLOTS, SAMP, E), BF16),
            pltpu.VMEM((SLOTS, SAMP, E), BF16),
            pltpu.VMEM((SAMP, WIDTH), BF16),
            pltpu.VMEM((TABLES, SAMP), jnp.int32),
            pltpu.VMEM((TABLES, SAMP), jnp.int32),
            pltpu.VMEM((4, 4) + whole, BF16),
            pltpu.VMEM((4,) + half, BF16),
            pltpu.VMEM((4,) + half, BF16),
            pltpu.VMEM((4,) + whole, BF16),
            pltpu.VMEM((4,) + whole, BF16),
            pltpu.VMEM((3,) + whole, BF16),
            pltpu.VMEM((2,) + half, BF16),
            pltpu.VMEM((2,) + whole, BF16),
            pltpu.VMEM(whole, BF16),
            pltpu.VMEM((4, 2, PAD, RANK), BF16),
            pltpu.SemaphoreType.DMA((N_GATHER,)),
            pltpu.SemaphoreType.DMA((N_GATHER,)),
            pltpu.SemaphoreType.DMA((N_REDUCE,)),
            pltpu.SemaphoreType.DMA((N_REDUCE,)),
            pltpu.SemaphoreType.DMA((9,)),
            pltpu.SemaphoreType.DMA,
            pltpu.SemaphoreType.DMA,
            pltpu.SemaphoreType.DMA,
            pltpu.SemaphoreType.DMA,
        ],
        compiler_params=pltpu.CompilerParams(
            collective_id=1, has_side_effects=True, vmem_limit_bytes=62 << 20
        ),
        name="cross_step",
    )(slots, index, pooled, shard, stacked, upstream, counts_a, dense, counts_b)


def local(
    pooled_b,
    dense_output_second,
    counts_b,
    slot_of,
    stacked_a,
    upstream_a,
    counts_a,
    down_projection,
    proj_up,
    cross_layer_bias,
):
    slots = slot_of[:TABLES]
    held = slots[None, :] == jnp.arange(SLOTS, dtype=jnp.int32)[:, None]
    index = jnp.sum(jnp.where(held, jnp.arange(1, TABLES + 1, dtype=jnp.int32), 0), axis=1)
    bias_row = jnp.pad(cross_layer_bias[None, :], ((0, 1), (0, RANK - ROWS)))
    shard = jnp.stack(
        [
            jnp.concatenate([down_projection, bias_row], axis=0),
            jnp.pad(jnp.transpose(proj_up), ((0, PAD - ROWS), (0, 0))),
        ]
    )
    crossed_b, dense_gradient, returned, sums = step(
        slots,
        index,
        pooled_b[0],
        shard,
        stacked_a,
        upstream_a,
        jnp.transpose(counts_a),
        dense_output_second,
        jnp.transpose(counts_b),
    )
    return (
        crossed_b,
        dense_gradient,
        returned[None],
        sums[0, :ROWS],
        jnp.transpose(sums[1, :ROWS]),
        sums[0, ROWS, :ROWS],
    )


def solution(mesh):
    return jax.shard_map(
        local,
        mesh=mesh,
        in_specs=(
            P("wide", None, "pair", None),
            P(("wide", "pair"), None),
            P(("wide", "pair"), None),
            P(),
            P(("wide", "pair"), None),
            P(("wide", "pair"), None),
            P(("wide", "pair"), None),
            P("wide", None),
            P(None, "wide"),
            P("wide"),
        ),
        out_specs=(
            P(("wide", "pair"), None),
            P(("wide", "pair"), None),
            P("wide", None, "pair", None),
            P("wide", None),
            P(None, "wide"),
            P("wide"),
        ),
        check_vma=False,
    )
```

time: 219 us -> 173 us (0.79)
  blocking collectives: 59.3 us -> 0 us
  Pallas kernels: 136 us -> 158 us
  starting transfers between devices: 5.72 us -> 0 us
  local copies, waits for them, and re-layouts: 16 us -> 11 us
    all_to_all x1 -> x0, blocking collectives: 59.3 us -> none  [local(): lax.all_to_all(slot_grad.reshape(SLOTS, 1, SAMP, E), 'wide', split_axis=0...]
    pallas_call x4 -> x1, Pallas kernels: 136 us -> 158 us  [step(): pl.pallas_call(step_kernel, out_shape=(jax.ShapeDtypeStruct((SAMP, WIDTH)...]
    unnamed x23 -> x5, local copies, waits for them, and re-layouts: 14.8 us -> 8.17 us
    all_to_all x1 -> x0, starting transfers between devices: 5.72 us -> none  [local(): lax.all_to_all(pooled_b, 'wide', split_axis=1, concat_axis=0, tiled=True)]
  transfers between devices with their start and end apart: 1 -> 0, of which waited for: 0 -> 0; matrix products, arithmetic and copies ran while one was open for 1% -> 0% of each run, Pallas kernels for 34% -> 0%
where the time goes in v2:
time: 173 us
  Pallas kernels  158 us (91%)
  local copies, waits for them, and re-layouts  11 us (6%)
  other arithmetic  2.79 us (2%)
    pallas_call x1, Pallas kernels, step(): pl.pallas_call(step_kernel, out_shape=(jax.ShapeDtypeStruct((SAMP, WIDTH)...  158 us
    unnamed x5, local copies, waits for them, and re-layouts  8.17 us

profile of v2, /device:TPU:1, one launch (start us, length us, event | category | flops | bytes accessed | tf_op | source)
XLA Modules:
  0.0 172.9 jit_solution(18071722647649070114)
XLA Ops:
  0.6 1.3 select_reduce_fusion.index
  1.9 0.9 fusion.2
  2.8 0.7 pad_maximum_fusion.shard
  3.4 158.4 %cross_step.1 = (bf16[256,3456]{1,0:T(8,128)(2,1)}, bf16[256,128]{1,0:T(8,128)(2,1)}, bf16[64,256,128]{2,1,0:T(8,128)(2,1)}, f32[2,56,512]{2,1,0:T(8,128)}) custom-call(s32[26]{0:T(128)} %bitcast.26, s32[64]{0:T(128)} %select_reduce_fusion.index, bf16[64,256,128]{2,1,0:T(8,128)(2,1)} %bitcast.19, bf16[2,56,512]{2,1,0:T(8,128)(2,1)} %pad_maximum_fusion.shard, ...), custom_call_target="tpu_custom_call" | custom-call | tf_op jit(solution)/shard_map/cross_step/pallas_call | solution.py:471
  161.9 1.7 slice_bitcast_fusion
  163.5 1.2 slice_bitcast_fusion.2
  164.7 0.0 copy-start
  164.7 2.8 %copy.19 = bf16[256,3456]{1,0:T(8,128)(2,1)} copy(bf16[256,3456]{1,0:T(8,128)(2,1)} %get-tuple-element.24) | data formatting | bytes 3538944
  167.5 0.0 copy-done
  167.5 0.6 copy.20
  168.2 4.7 %copy.21 = bf16[1,64,256,128]{3,2,1,0:T(8,128)(2,1)} copy(bf16[1,64,256,128]{3,2,1,0:T(8,128)(2,1)} %bitcast.20) | data formatting | bytes 8388608
  (1 shorter events, 0.0 us)
Async XLA Ops:
  164.7 2.8 %copy-start = (bf16[256,128]{1,0:T(8,128)(2,1)S(1)}, bf16[256,128]{1,0:T(8,128)(2,1)}, u32[]{:S(2)}) copy-start(bf16[256,128]{1,0:T(8,128)(2,1)} %get-tuple-element.25) | copy-start | bytes 196612

commit v3 on v2

--- a/solution.py
+++ b/solution.py
@@ -93,9 +93,9 @@
     return (m, z, x, yh * 2 + c) if m == 0 else (m, x, z, yh * 2 + c)
 
 
-def step_kernel(slots, index, pooled, shard, stacked_h, upstream_h, counts_a_h, dense_h, counts_b_h,
+def step_kernel(slots, pooled, down_h, up_h, bias_h, stacked_h, upstream_h, counts_a_h, dense_h, counts_b_h,
                 crossed_h, dense_g, returned, out,
-                full, v, u, bias, stacked, upstream, pg, gv, gu, gb, tg, snd, arrived, st, counts_a,
+                index, raw, raw_bias, shard, full, v, u, bias, stacked, upstream, pg, gv, gu, gb, tg, snd, arrived, st, counts_a,
                 counts_b, sibling, mid_p, mid_m, end_p, end_m, total, imid, iend, inner, last,
                 gsend, grecv, rsend, rrecv, local_sem, bsend, brecv, asend, arecv):
     place_of = place()
@@ -125,7 +125,7 @@
         load(dense_h, st.at[:, pl.ds(0, E)], 4),
     ]
     mine_b = load(pooled.at[me], arrived.at[me], 5)
-    mine_w = load(shard.at[c], full.at[c, b, a, k], 6)
+    raws = [load(down_h, raw.at[0], 6), load(up_h, raw.at[1], 9), load(bias_h, raw_bias, 10)]
 
     barrier = pltpu.get_barrier_semaphore()
 
@@ -141,6 +141,12 @@
             pl.semaphore_signal(
                 barrier, inc=1, device_id=device(x, yy // 2, yy % 2, z, i), device_id_type=MESH
             )
+    shard[...] = jnp.zeros_like(shard)
+    for cp in raws:
+        cp.wait()
+    for i in range(2):
+        shard[i, 0:ROWS] = raw[i]
+    shard[0, ROWS : ROWS + 1, 0:ROWS] = raw_bias[...]
     pl.semaphore_wait(barrier, SLOTS - 1 + 4)
 
     fed = [0, 0]
@@ -194,7 +200,15 @@
         s1.append(gcopy(shard.at[i], full.at[i, bi, ai, k], part[i], 1 + (c + i) % 2))
     s1.append(gcopy(shard.at[o], full.at[o, a, b, k], sib, 0))
     feed_b(FEED_B[0])
-    mine_w.wait()
+
+    @pl.loop(0, SLOTS)
+    def _(s):
+        held = jnp.int32(0)
+        for t in range(TABLES):
+            held = jnp.where(slots[t] == s, t + 1, held)
+        index[s] = held
+
+    full[c, b, a, k] = shard[c]
     for cp in s1:
         cp.wait_recv()
     a_m, a_p, a_o = (a + 3) % 4, (a + 1) % 4, (a + 2) % 4
@@ -462,7 +476,7 @@
     await_exchange(asend, arecv, returned)
 
 
-def step(slots, index, pooled, shard, stacked, upstream, counts_a, dense, counts_b):
+def step(slots, pooled, down, up, bias, stacked, upstream, counts_a, dense, counts_b):
     smem = pl.BlockSpec(memory_space=pltpu.SMEM)
     vmem = pl.BlockSpec(memory_space=pltpu.VMEM)
     anywhere = pl.BlockSpec(memory_space=pl.ANY)
@@ -476,9 +490,13 @@
             jax.ShapeDtypeStruct((SLOTS, SAMP, E), BF16),
             jax.ShapeDtypeStruct((2, PAD, RANK), F32),
         ),
-        in_specs=[smem] * 2 + [anywhere] * 7,
+        in_specs=[smem] + [anywhere] * 9,
         out_specs=[anywhere, vmem, anywhere, vmem],
         scratch_shapes=[
+            pltpu.SMEM((SLOTS,), jnp.int32),
+            pltpu.VMEM((2, ROWS, RANK), BF16),
+            pltpu.VMEM((1, ROWS), BF16),
+            pltpu.VMEM((2, PAD, RANK), BF16),
             pltpu.VMEM((2, 4, 4, 4, PAD, RANK), BF16),
             pltpu.VMEM((WIDTH, RANK), BF16),
             pltpu.VMEM((WIDTH, RANK), BF16),
@@ -509,7 +527,7 @@
             pltpu.SemaphoreType.DMA((N_GATHER,)),
             pltpu.SemaphoreType.DMA((N_REDUCE,)),
             pltpu.SemaphoreType.DMA((N_REDUCE,)),
-            pltpu.SemaphoreType.DMA((9,)),
+            pltpu.SemaphoreType.DMA((11,)),
             pltpu.SemaphoreType.DMA,
             pltpu.SemaphoreType.DMA,
             pltpu.SemaphoreType.DMA,
@@ -519,7 +537,76 @@
             collective_id=1, has_side_effects=True, vmem_limit_bytes=62 << 20
         ),
         name="cross_step",
-    )(slots, index, pooled, shard, stacked, upstream, counts_a, dense, counts_b)
+    )(slots, pooled, down, up, bias, stacked, upstream, counts_a, dense, counts_b)
+
+
+PIECES = 8
+
+
+def write_kernel(crossed, dense, returned, sums, crossed_o, dense_o, returned_o, down_o, up_o,
+                 bias_o, crossed_v, dense_v, returned_v, sums_v, down_v, up_v, rsem, wsem):
+    part = SLOTS // PIECES
+    n = [0]
+
+    def pair(src, mid, dst):
+        i = n[0]
+        n[0] += 1
+        read = pltpu.make_async_copy(src, mid, rsem.at[i])
+        read.start()
+        return read, pltpu.make_async_copy(mid, dst, wsem.at[i])
+
+    small = pltpu.make_async_copy(sums, sums_v, rsem.at[PIECES + 2])
+    small.start()
+    pairs = [pair(crossed, crossed_v, crossed_o), pair(dense, dense_v, dense_o)]
+    for i in range(PIECES):
+        at = pl.ds(part * i, part)
+        pairs.append(pair(returned.at[at], returned_v.at[at], returned_o.at[at]))
+    small.wait()
+    down_v[...] = sums_v[0, 0:ROWS]
+    up_v[...] = sums_v[1, 0:ROWS]
+    bias_o[...] = sums_v[0, ROWS, 0:ROWS]
+    writes = [
+        pltpu.make_async_copy(down_v, down_o, wsem.at[PIECES + 2]),
+        pltpu.make_async_copy(up_v, up_o, wsem.at[PIECES + 3]),
+    ]
+    for cp in writes:
+        cp.start()
+    for read, write in pairs:
+        read.wait()
+        write.start()
+        writes.append(write)
+    for cp in writes:
+        cp.wait()
+
+
+def write_out(crossed, dense, returned, sums):
+    vmem = pl.BlockSpec(memory_space=pltpu.VMEM)
+    anywhere = pl.BlockSpec(memory_space=pl.ANY)
+    return pl.pallas_call(
+        write_kernel,
+        out_shape=(
+            jax.ShapeDtypeStruct((SAMP, WIDTH), BF16),
+            jax.ShapeDtypeStruct((SAMP, E), BF16),
+            jax.ShapeDtypeStruct((SLOTS, SAMP, E), BF16),
+            jax.ShapeDtypeStruct((ROWS, RANK), F32),
+            jax.ShapeDtypeStruct((ROWS, RANK), F32),
+            jax.ShapeDtypeStruct((ROWS,), F32),
+        ),
+        in_specs=[anywhere] * 4,
+        out_specs=[anywhere] * 5 + [vmem],
+        scratch_shapes=[
+            pltpu.VMEM((SAMP, WIDTH), BF16),
+            pltpu.VMEM((SAMP, E), BF16),
+            pltpu.VMEM((SLOTS, SAMP, E), BF16),
+            pltpu.VMEM((2, PAD, RANK), F32),
+            pltpu.VMEM((ROWS, RANK), F32),
+            pltpu.VMEM((ROWS, RANK), F32),
+            pltpu.SemaphoreType.DMA((PIECES + 4,)),
+            pltpu.SemaphoreType.DMA((PIECES + 4,)),
+        ],
+        compiler_params=pltpu.CompilerParams(vmem_limit_bytes=62 << 20),
+        name="write_out",
+    )(crossed, dense, returned, sums)
 
 
 def local(
@@ -535,33 +622,27 @@
     cross_layer_bias,
 ):
     slots = slot_of[:TABLES]
-    held = slots[None, :] == jnp.arange(SLOTS, dtype=jnp.int32)[:, None]
-    index = jnp.sum(jnp.where(held, jnp.arange(1, TABLES + 1, dtype=jnp.int32), 0), axis=1)
-    bias_row = jnp.pad(cross_layer_bias[None, :], ((0, 1), (0, RANK - ROWS)))
-    shard = jnp.stack(
-        [
-            jnp.concatenate([down_projection, bias_row], axis=0),
-            jnp.pad(jnp.transpose(proj_up), ((0, PAD - ROWS), (0, 0))),
-        ]
-    )
-    crossed_b, dense_gradient, returned, sums = step(
-        slots,
-        index,
-        pooled_b[0],
-        shard,
-        stacked_a,
-        upstream_a,
-        jnp.transpose(counts_a),
-        dense_output_second,
-        jnp.transpose(counts_b),
+    crossed_b, dense_gradient, returned, grad_down, grad_up, grad_bias = write_out(
+        *step(
+            slots,
+            pooled_b[0],
+            down_projection,
+            jnp.transpose(proj_up),
+            cross_layer_bias[None, :],
+            stacked_a,
+            upstream_a,
+            jnp.transpose(counts_a),
+            dense_output_second,
+            jnp.transpose(counts_b),
+        )
     )
     return (
         crossed_b,
         dense_gradient,
         returned[None],
-        sums[0, :ROWS],
-        jnp.transpose(sums[1, :ROWS]),
-        sums[0, ROWS, :ROWS],
+        grad_down,
+        jnp.transpose(grad_up),
+        grad_bias,
     )
 
 

time: 173 us -> 164 us (0.948)
  local copies, waits for them, and re-layouts: 11 us -> 0 us
  Pallas kernels: 158 us -> 164 us
  other arithmetic: 2.79 us -> 0 us
    unnamed x5 -> x0, local copies, waits for them, and re-layouts: 8.17 us -> none
    pallas_call x0 -> x1, Pallas kernels: none -> 5.32 us  [write_out(): pl.pallas_call(write_kernel, out_shape=(jax.ShapeDtypeStruct((SAMP, WIDTH...]
where the time goes in v3:
time: 164 us
  Pallas kernels  164 us (100%)
    pallas_call x1, Pallas kernels, step(): pl.pallas_call(step_kernel, out_shape=(jax.ShapeDtypeStruct((SAMP, WIDTH)...  158 us
    pallas_call x1, Pallas kernels, write_out(): pl.pallas_call(write_kernel, out_shape=(jax.ShapeDtypeStruct((SAMP, WIDTH...  5.32 us

profile of v3, /device:TPU:1, one launch (start us, length us, event | category | flops | bytes accessed | tf_op | source)
XLA Modules:
  0.0 164.3 jit_solution(3491790281997447623)
XLA Ops:
  0.6 158.3 %cross_step.1 = (bf16[256,3456]{1,0:T(8,128)(2,1)}, bf16[256,128]{1,0:T(8,128)(2,1)}, bf16[64,256,128]{2,1,0:T(8,128)(2,1)}, f32[2,56,512]{2,1,0:T(8,128)}) custom-call(s32[26]{0:T(128)} %bitcast.12, bf16[64,256,128]{2,1,0:T(8,128)(2,1)} %bitcast.8, bf16[54,512]{1,0:T(8,128)(2,1)} %down_h.1, bf16[54,512]{1,0:T(8,128)(2,1)} %bitcast.9, ...), custom_call_target="tpu_custom_call" | custom-call | tf_op jit(solution)/shard_map/cross_step/pallas_call | solution.py:485
  158.9 5.3 %write_out.1 = (bf16[256,3456]{1,0:T(8,128)(2,1)}, bf16[256,128]{1,0:T(8,128)(2,1)}, bf16[64,256,128]{2,1,0:T(8,128)(2,1)}, f32[54,512]{1,0:T(8,128)}, f32[54,512]{1,0:T(8,128)}, /*index=5*/f32[54]{0:T(128)}) custom-call(bf16[256,3456]{1,0:T(8,128)(2,1)} %get-tuple-element.16.crossed, bf16[256,128]{1,0:T(8,128)(2,1)} %get-tuple-element.17.dense, ...), custom_call_target="tpu_custom_call" | custom-call | tf_op jit(solution)/shard_map/write_out/pallas_call | solution.py:585

commit v4 on v3

--- a/solution.py
+++ b/solution.py
@@ -76,8 +76,8 @@
 ORDER = exchange_order()
 N_GATHER = 3 + 4 + 16 + 16
 N_REDUCE = 16 + 8 + 8 + 4 + 7
-FEED_B = (0, 4, 4, 4, 4, 4, 4, 4, 4)
-FEED_A = (8, 4, 4, 4, 4, 4, 4, 4, 4, 4)
+FEED_B = (0, 8, 5, 5, 5, 5, 5, 5, 5)
+FEED_A = (4, 6, 6, 6, 6, 8, 8)
 
 
 def target(me, offset):
@@ -97,7 +97,7 @@
                 crossed_h, dense_g, returned, out,
                 index, raw, raw_bias, shard, full, v, u, bias, stacked, upstream, pg, gv, gu, gb, tg, snd, arrived, st, counts_a,
                 counts_b, sibling, mid_p, mid_m, end_p, end_m, total, imid, iend, inner, last,
-                gsend, grecv, rsend, rrecv, local_sem, bsend, brecv, asend, arecv):
+                gsend, grecv, rsend, rrecv, local_sem, bsend, brecv, asend, arecv, x_sem, z_sem):
     place_of = place()
     x, yh, yl, z, c = place_of
     me = lax.axis_index("wide")
@@ -128,26 +128,26 @@
     raws = [load(down_h, raw.at[0], 6), load(up_h, raw.at[1], 9), load(bias_h, raw_bias, 10)]
 
     barrier = pltpu.get_barrier_semaphore()
-
-    @pl.loop(0, SLOTS)
-    def _(i):
-        @pl.when(i != me)
-        def _():
-            pl.semaphore_signal(barrier, inc=1, device_id=(i, yl), device_id_type=MESH)
-
-    for d in (1, 3):
-        for i in range(2):
-            yy = (y + d) % 4
-            pl.semaphore_signal(
-                barrier, inc=1, device_id=device(x, yy // 2, yy % 2, z, i), device_id_type=MESH
-            )
+    x_line = [device((x + d) % 4, yh, yl, z, c) for d in range(1, 4)]
+    z_line = [device(x, yh, yl, (z + d) % 4, c) for d in range(1, 4)]
+    column = []
+    for d in range(1, 4):
+        yy = (y + d) % 4
+        column += [device(x, yy // 2, yy % 2, z, i) for i in range(2)]
+
+    def greet(sem, devices):
+        for to in devices:
+            pl.semaphore_signal(sem, inc=1, device_id=to, device_id_type=MESH)
+
+    greet(barrier, [sib] + x_line + z_line + column)
     shard[...] = jnp.zeros_like(shard)
     for cp in raws:
         cp.wait()
     for i in range(2):
         shard[i, 0:ROWS] = raw[i]
     shard[0, ROWS : ROWS + 1, 0:ROWS] = raw_bias[...]
-    pl.semaphore_wait(barrier, SLOTS - 1 + 4)
+    pl.semaphore_wait(barrier, 13)
+    greet(x_sem, x_line)
 
     fed = [0, 0]
 
@@ -199,7 +199,6 @@
         bi, ai = (z, x) if i == 0 else (x, z)
         s1.append(gcopy(shard.at[i], full.at[i, bi, ai, k], part[i], 1 + (c + i) % 2))
     s1.append(gcopy(shard.at[o], full.at[o, a, b, k], sib, 0))
-    feed_b(FEED_B[0])
 
     @pl.loop(0, SLOTS)
     def _(s):
@@ -209,6 +208,8 @@
         index[s] = held
 
     full[c, b, a, k] = shard[c]
+    pl.semaphore_wait(x_sem, 3)
+    greet(z_sem, z_line)
     for cp in s1:
         cp.wait_recv()
     a_m, a_p, a_o = (a + 3) % 4, (a + 1) % 4, (a + 2) % 4
@@ -232,7 +233,8 @@
     up = ring(b, a, a_next, 3)
     down = ring(b, a, a_prev, 4)
     out_ring(0, a)
-    feed_b(FEED_B[1])
+    pl.semaphore_wait(z_sem, 3)
+    feed_b(FEED_B[0] + FEED_B[1])
     up.wait_recv()
     up2 = ring(b, a_m, a_next, 5, lo)
     out_ring(1, a_m)
@@ -532,6 +534,8 @@
             pltpu.SemaphoreType.DMA,
             pltpu.SemaphoreType.DMA,
             pltpu.SemaphoreType.DMA,
+            pltpu.SemaphoreType.REGULAR,
+            pltpu.SemaphoreType.REGULAR,
         ],
         compiler_params=pltpu.CompilerParams(
             collective_id=1, has_side_effects=True, vmem_limit_bytes=62 << 20

time: 164 us -> 159 us (0.970); the launches traced: 164 us -> 157 us
  Pallas kernels: 164 us -> 156 us
    pallas_call x1, Pallas kernels: 158 us -> 151 us  [step(): pl.pallas_call(step_kernel, out_shape=(jax.ShapeDtypeStruct((SAMP, WIDTH)...]
where the time goes in v4:
time: 159 us; the launch traced here: 157 us
  Pallas kernels  156 us (98%)
    pallas_call x1, Pallas kernels, step(): pl.pallas_call(step_kernel, out_shape=(jax.ShapeDtypeStruct((SAMP, WIDTH)...  151 us
    pallas_call x1, Pallas kernels, write_out(): pl.pallas_call(write_kernel, out_shape=(jax.ShapeDtypeStruct((SAMP, WIDTH...  5.32 us

profile of v4, /device:TPU:1, one launch (start us, length us, event | category | flops | bytes accessed | tf_op | source)
XLA Modules:
  0.0 156.9 jit_solution(6479905947769543786)
XLA Ops:
  0.6 151.0 %cross_step.1 = (bf16[256,3456]{1,0:T(8,128)(2,1)}, bf16[256,128]{1,0:T(8,128)(2,1)}, bf16[64,256,128]{2,1,0:T(8,128)(2,1)}, f32[2,56,512]{2,1,0:T(8,128)}) custom-call(s32[26]{0:T(128)} %bitcast.12, bf16[64,256,128]{2,1,0:T(8,128)(2,1)} %bitcast.8, bf16[54,512]{1,0:T(8,128)(2,1)} %down_h.1, bf16[54,512]{1,0:T(8,128)(2,1)} %bitcast.9, ...), custom_call_target="tpu_custom_call" | custom-call | tf_op jit(solution)/shard_map/cross_step/pallas_call | solution.py:487
  151.6 5.3 %write_out.1 = (bf16[256,3456]{1,0:T(8,128)(2,1)}, bf16[256,128]{1,0:T(8,128)(2,1)}, bf16[64,256,128]{2,1,0:T(8,128)(2,1)}, f32[54,512]{1,0:T(8,128)}, f32[54,512]{1,0:T(8,128)}, /*index=5*/f32[54]{0:T(128)}) custom-call(bf16[256,3456]{1,0:T(8,128)(2,1)} %get-tuple-element.16.crossed, bf16[256,128]{1,0:T(8,128)(2,1)} %get-tuple-element.17.dense, ...), custom_call_target="tpu_custom_call" | custom-call | tf_op jit(solution)/shard_map/write_out/pallas_call | solution.py:589

commit v5 on v4

--- a/solution.py
+++ b/solution.py
@@ -232,21 +232,19 @@
 
     up = ring(b, a, a_next, 3)
     down = ring(b, a, a_prev, 4)
+    far_a = ring(b, a, along_a(x, yh, yl, z, c, 2), 5)
     out_ring(0, a)
     pl.semaphore_wait(z_sem, 3)
     feed_b(FEED_B[0] + FEED_B[1])
     up.wait_recv()
-    up2 = ring(b, a_m, a_next, 5, lo)
     out_ring(1, a_m)
     down.wait_recv()
-    down2 = ring(b, a_p, a_prev, 6, hi)
     out_ring(2, a_p)
     over(b, a, 0)
     over(b, a_m, 1)
     over(b, a_p, 2)
     feed_b(FEED_B[2])
-    up2.wait_recv()
-    down2.wait_recv()
+    far_a.wait_recv()
     out_ring(3, a_o)
     over(b, a_o, 3)
     feed_b(FEED_B[3])
@@ -391,18 +389,11 @@
         return own + end_m[j].astype(F32)
 
     total[0] = summed(0, 2).astype(BF16)
-    fp = rcopy(total.at[0, lo], imid.at[0], a_next)
-    fm = rcopy(total.at[0, hi], imid.at[1], a_prev)
+    far_a = rcopy(total.at[0], imid, along_a(x, yh, yl, z, c, 2))
     feed_a(FEED_A[5])
-    near_p = summed(1, 1)
-    near_m = summed(2, 3)
-    total[1, hi] = near_p[2:4].astype(BF16)
-    total[2, lo] = near_m[0:2].astype(BF16)
-    fp.wait_recv()
-    total[1, lo] = (near_p[0:2] + imid[0].astype(F32)).astype(BF16)
+    total[1] = summed(1, 1).astype(BF16)
     gp = rcopy(total.at[1], iend.at[0], a_next)
-    fm.wait_recv()
-    total[2, hi] = (near_m[2:4] + imid[1].astype(F32)).astype(BF16)
+    total[2] = summed(2, 3).astype(BF16)
     gm = rcopy(total.at[2], iend.at[1], a_prev)
     feed_a(FEED_A[6])
     own = summed(3, 0)
@@ -410,6 +401,8 @@
     own = own + iend[0].astype(F32)
     gm.wait_recv()
     own = own + iend[1].astype(F32)
+    far_a.wait_recv()
+    own = own + imid[...].astype(F32)
     inner[...] = own.astype(BF16)
     base = m[0]
     for d in range(1, 4):
@@ -521,7 +514,7 @@
             pltpu.VMEM((4,) + whole, BF16),
             pltpu.VMEM((4,) + whole, BF16),
             pltpu.VMEM((3,) + whole, BF16),
-            pltpu.VMEM((2,) + half, BF16),
+            pltpu.VMEM(whole, BF16),
             pltpu.VMEM((2,) + whole, BF16),
             pltpu.VMEM(whole, BF16),
             pltpu.VMEM((4, 2, PAD, RANK), BF16),

time: 159 us -> 158 us (level); the launches traced: 157 us -> 158 us
  no operation moved by 1% of the time
where the time goes in v5:
time: 158 us
  Pallas kernels  157 us (99%)
    pallas_call x1, Pallas kernels, step(): pl.pallas_call(step_kernel, out_shape=(jax.ShapeDtypeStruct((SAMP, WIDTH)...  152 us
    pallas_call x1, Pallas kernels, write_out(): pl.pallas_call(write_kernel, out_shape=(jax.ShapeDtypeStruct((SAMP, WIDTH...  5.32 us

profile of v5, /device:TPU:1, one launch (start us, length us, event | category | flops | bytes accessed | tf_op | source)
XLA Modules:
  0.0 157.6 jit_solution(10636854432762894763)
XLA Ops:
  0.6 151.7 %cross_step.1 = (bf16[256,3456]{1,0:T(8,128)(2,1)}, bf16[256,128]{1,0:T(8,128)(2,1)}, bf16[64,256,128]{2,1,0:T(8,128)(2,1)}, f32[2,56,512]{2,1,0:T(8,128)}) custom-call(s32[26]{0:T(128)} %bitcast.12, bf16[64,256,128]{2,1,0:T(8,128)(2,1)} %bitcast.8, bf16[54,512]{1,0:T(8,128)(2,1)} %down_h.1, bf16[54,512]{1,0:T(8,128)(2,1)} %bitcast.9, ...), custom_call_target="tpu_custom_call" | custom-call | tf_op jit(solution)/shard_map/cross_step/pallas_call | solution.py:480
  152.3 5.3 %write_out.1 = (bf16[256,3456]{1,0:T(8,128)(2,1)}, bf16[256,128]{1,0:T(8,128)(2,1)}, bf16[64,256,128]{2,1,0:T(8,128)(2,1)}, f32[54,512]{1,0:T(8,128)}, f32[54,512]{1,0:T(8,128)}, /*index=5*/f32[54]{0:T(128)}) custom-call(bf16[256,3456]{1,0:T(8,128)(2,1)} %get-tuple-element.16.crossed, bf16[256,128]{1,0:T(8,128)(2,1)} %get-tuple-element.17.dense, ...), custom_call_target="tpu_custom_call" | custom-call | tf_op jit(solution)/shard_map/write_out/pallas_call | solution.py:582
